TPU v7x, 512 devices: a whole 4x4x16 slice. The times are simulated.
512 devices in a mesh: space: 128 (over y, z, core), level: 4 (over x).
Axes of the slice: x: 4, y: 4, z: 16, core: 2. Of those that a mesh axis runs over, the one named last changes fastest.
Arguments:
- grid_latent: bfloat16 [65536, 512], P('space'), may hold values from -6 to 6
- mesh_latent: bfloat16 [4, 1024, 512], P('level', 'space'), may hold values from -6 to 6
- grid_output_cotangent: bfloat16 [65536, 512], P('space'), may hold values from -6 to 6
- w_send: bfloat16 [512, 512], replicated, may hold values from -0.25 to 0.25
- w_recv: bfloat16 [512, 512], replicated, may hold values from -0.25 to 0.25
- output_weight: bfloat16 [512, 512], replicated, may hold values from -0.25 to 0.25
- hidden_layer_bias: float32 [512], replicated, may hold values from -4 to 4
- output_norm_gain: float32 [512], replicated, may hold values from 0.1 to 1.9
- edge_sender: int32 [4, 262144], P('level', 'space'), may hold values from 0 to 23
- edge_receiver: int32 [4, 262144], P('level', 'space'), may hold values from 0 to 511
- edge_live: int32 [4, 262144], P('level', 'space'), may hold values 0 or 1
Outputs:
- d_grid: float32 [65536, 512], P(('space', 'level'))
- d_mesh: float32 [4, 1024, 512], P('level', 'space')
- d_w_send: bfloat16 [512, 512], replicated
- d_w_recv: bfloat16 [512, 512], replicated
- d_w_out: bfloat16 [512, 512], replicated
- d_bias: float32 [512], replicated
- d_gain: float32 [512], replicated
All inputs are finite; a program needn't handle non-finite values. No bound on the sum of `edge_live` on one device may be relied on, other than what follows from the above.
Results may differ from a plain program's by a relative error of at most 0.012.
Values may be sent and summed in bfloat16 or wider, within the bound.
A program may use at most 64 MiB of HBM per device.

v0:
```python
import jax
import jax.numpy as jnp
from jax import lax
from jax.sharding import PartitionSpec as P


def with_halo(cells, sides, width):
    for axis, dim in sides:
        count = lax.axis_size(axis)
        ends = count - 1
        head = lax.slice_in_dim(cells, 0, width, axis=dim)
        tail = lax.slice_in_dim(cells, cells.shape[dim] - width, cells.shape[dim], axis=dim)
        cells = jnp.concatenate(
            [
                lax.ppermute(tail, axis, [(i, (i + 1) % count) for i in range(ends)]),
                cells,
                lax.ppermute(head, axis, [((i + 1) % count, i) for i in range(ends)]),
            ],
            axis=dim,
        )
    return cells


def from_behind(block, axis, distance):
    devices = range(lax.axis_size(axis))
    route = [(i - distance, i) for i in devices if i - distance in devices]
    return lax.ppermute(block, axis, route)


def in_blocks(value, dim, peers):
    before, after = (value.shape[:dim], value.shape[dim + 1 :])
    return jnp.moveaxis(value.reshape(*before, peers, -1, *after), dim, 0)


def summed_on_arrival(value, axis, dim):
    peers = lax.axis_size(axis)
    tiles = lax.all_to_all(in_blocks(value, dim, peers), axis, 0, 0, tiled=True)
    return jnp.sum(tiles.astype(jnp.float32), axis=0)


def edge_reverse_step(
    sending_rows,
    receiver_rows,
    cotangent_lines,
    slot_active_flags,
    output_weight,
    hidden_layer_bias,
    output_norm_gain,
):
    preact = sending_rows + receiver_rows + hidden_layer_bias
    hidden = jax.nn.silu(preact).astype(jnp.bfloat16)
    outer = jnp.dot(hidden, output_weight, preferred_element_type=jnp.float32)
    center = outer - jnp.mean(outer, axis=-1, keepdims=True)
    inv_scale = lax.rsqrt(jnp.mean(center * center, axis=-1, keepdims=True) + 1e-05)
    normed = center * inv_scale
    incoming_gradient = cotangent_lines.astype(jnp.float32) * slot_active_flags[:, None].astype(
        jnp.float32
    )
    scaled = incoming_gradient * output_norm_gain
    d_outer = inv_scale * (
        scaled
        - jnp.mean(scaled, axis=-1, keepdims=True)
        - normed * jnp.mean(scaled * normed, axis=-1, keepdims=True)
    )
    d_outer_b = d_outer.astype(jnp.bfloat16)
    w_out_grad = jnp.dot(hidden.T, d_outer_b, preferred_element_type=jnp.float32)
    d_hidden = jnp.dot(d_outer_b, output_weight.T, preferred_element_type=jnp.float32)
    sigmoid = jax.nn.sigmoid(preact)
    preactivation_gradient = d_hidden * sigmoid * (1.0 + preact * (1.0 - sigmoid))
    return (
        preactivation_gradient,
        w_out_grad,
        jnp.sum(preactivation_gradient, axis=0),
        jnp.sum(incoming_gradient * normed, axis=0),
    )


def body(
    grid_latent,
    mesh_latent,
    grid_output_cotangent,
    w_send,
    w_recv,
    output_weight,
    hidden_layer_bias,
    output_norm_gain,
    edge_sender,
    edge_receiver,
    edge_live,
):
    shards = lax.axis_size("space")
    width = grid_latent.shape[1]
    grid_rows = grid_latent.shape[0]
    mesh_rows = mesh_latent.shape[1]
    slots = edge_sender.shape[1]
    sender_local = edge_sender[0]
    receiver_index = edge_receiver[0]
    band = lax.axis_index("space")
    window = sender_local // mesh_rows
    target = band + window - 1
    inside = (target >= 0) & (target < shards)
    window = jnp.where(inside, window, 1)
    table_row = window * mesh_rows + sender_local % mesh_rows
    proj_send = jnp.dot(mesh_latent[0], w_send, preferred_element_type=jnp.float32).astype(
        jnp.bfloat16
    )
    projected_receiver = jnp.dot(grid_latent, w_recv, preferred_element_type=jnp.float32)
    table = with_halo(proj_send, (("space", 0),), mesh_rows)
    sending_rows = table[table_row]
    block = 512
    blocks = slots // block

    def run_block(operands):
        rows_send, rows_recv, rows_cot, rows_live = operands
        return edge_reverse_step(
            rows_send.astype(jnp.float32),
            rows_recv,
            rows_cot,
            rows_live,
            output_weight,
            hidden_layer_bias,
            output_norm_gain,
        )

    operands = (
        sending_rows.reshape(blocks, block, width),
        projected_receiver[receiver_index].reshape(blocks, block, width),
        grid_output_cotangent[receiver_index].reshape(blocks, block, width),
        edge_live[0].reshape(blocks, block),
    )
    d_pre_blocks, wout_blocks, bias_blocks, gain_blocks = lax.map(run_block, operands)
    preactivation_gradient = d_pre_blocks.reshape(slots, width)
    output_weight_piece = jnp.sum(wout_blocks, axis=0)
    bias_piece = jnp.sum(bias_blocks, axis=0)
    gain_piece = jnp.sum(gain_blocks, axis=0)
    table_grads = jax.ops.segment_sum(preactivation_gradient, table_row, num_segments=3 * mesh_rows)
    below = table_grads[:mesh_rows]
    above = table_grads[2 * mesh_rows :]
    from_below = from_behind(above, "space", 1)
    from_above = from_behind(below, "space", -1)
    mesh_acc = table_grads[mesh_rows : 2 * mesh_rows] + from_below + from_above
    grid_local = jax.ops.segment_sum(preactivation_gradient, receiver_index, num_segments=grid_rows)
    share = grid_rows // lax.axis_size("level")
    offset = lax.axis_index("level") * share
    grid_acc = summed_on_arrival(grid_local.astype(jnp.bfloat16), "level", 0)
    grid_part = lax.dynamic_slice_in_dim(grid_latent, offset, share, 0)
    mesh_sum = mesh_acc.astype(jnp.bfloat16)
    grid_sum = grid_acc.astype(jnp.bfloat16)
    d_mesh = jnp.dot(mesh_sum, w_send.T, preferred_element_type=jnp.float32)[None]
    d_grid = jnp.dot(grid_sum, w_recv.T, preferred_element_type=jnp.float32)
    wsend_part = jnp.dot(mesh_latent[0].T, mesh_sum, preferred_element_type=jnp.float32)
    wrecv_part = jnp.dot(grid_part.T, grid_sum, preferred_element_type=jnp.float32)
    totals = lax.psum(
        (wsend_part, wrecv_part, output_weight_piece, bias_piece, gain_piece), ("space", "level")
    )
    d_w_send = totals[0].astype(jnp.bfloat16)
    d_w_recv = totals[1].astype(jnp.bfloat16)
    d_w_out = totals[2].astype(jnp.bfloat16)
    d_bias = totals[3]
    d_gain = totals[4]
    return (d_grid, d_mesh, d_w_send, d_w_recv, d_w_out, d_bias, d_gain)


def solution(mesh):
    return jax.shard_map(
        body,
        mesh=mesh,
        in_specs=(
            P("space", None),
            P("level", "space", None),
            P("space", None),
            P(),
            P(),
            P(),
            P(),
            P(),
            P("level", "space"),
            P("level", "space"),
            P("level", "space"),
        ),
        out_specs=(P(("space", "level"), None), P("level", "space", None), P(), P(), P(), P(), P()),
        check_vma=False,
    )
```

profile of v0, /device:TPU:1, one launch (start us, length us, event | category | flops | bytes accessed | tf_op | source)
XLA Modules:
  0.0 320.6 jit_solution(17864061252349421439)
XLA Ops:
  0.6 1.3 convolution_convert_fusion
  1.9 8.8 %collective-permute-start.1 = (bf16[8,512]{1,0:T(8,128)(2,1)S(1)}, bf16[8,512]{1,0:T(8,128)(2,1)S(1)}, u32[]{:S(2)}, u32[]{:S(2)}) collective-permute-start(bf16[8,512]{1,0:T(8,128)(2,1)S(1)} %convolution_convert_fusion), channel_id=1, source_target_pairs={{4,0},{8,4},{12,8},{16,12},{20,16},{24,20},{28,24},{32,28},{36,32}... | collective-permute-start | bytes 24584 | tf_op jit(solution)/shard_map/ppermute | solution.py:17
  10.7 1.9 collective-permute-start
  14.1 1.6 fusion.27
  16.3 1.4 reduce.4
  17.7 9.2 %gather_fusion.2 = bf16[2048,512]{1,0:T(8,128)(2,1)} fusion(bf16[512,512]{1,0:T(8,128)(2,1)S(1)} %copy-done, s32[2048]{0:T(1024)S(1)} %broadcast_clamp_fusion), kind=kCustom, calls=%fused_computation.2 | custom fusion | bytes 4202496 | tf_op jit(solution)/shard_map/gather | solution.py:128
  26.9 8.9 %gather_fusion.1 = f32[2048,512]{1,0:T(8,128)} fusion(f32[512,512]{1,0:T(8,128)S(1)} %fusion.27, s32[2048]{0:T(1024)S(1)} %broadcast_clamp_fusion), kind=kCustom, calls=%fused_computation.1 | custom fusion | bytes 8396800 | tf_op jit(solution)/shard_map/gather | solution.py:127
  35.8 9.2 %gather_fusion = bf16[2048,512]{1,0:T(8,128)(2,1)} fusion(bf16[24,512]{1,0:T(8,128)(2,1)S(1)} %pad_maximum_fusion, s32[2048]{0:T(1024)S(1)} %broadcast_clamp_fusion.1), kind=kCustom, calls=%fused_computation | custom fusion | bytes 4202496 | tf_op jit(solution)/shard_map/gather | solution.py:109
  45.0 37.2 %while.16 = (s32[]{:T(128)}, f32[4,512,512]{2,1,0:T(8,128)}, f32[4,512,512]{2,1,0:T(8,128)}, f32[4,512]{1,0:T(4,128)S(1)}, f32[4,512]{1,0:T(4,128)S(1)}, /*index...) while((s32[]{:T(128)}, f32[4,512,512]{2,1,0:T(8,128)}, ...), condition=%wide.region_7.8_spmd, body=%wide.region_0.7_spmd.sunk | while | flops 816840704 | bytes 18942132 | solution.py:131
  45.1 1.7 multiply_convert_fusion.2
  49.6 1.6 fusion.63
  51.2 3.0 bitcast_dynamic-update-slice_fusion.2
  54.4 1.7 multiply_convert_fusion.2
  56.1 1.1 constant_dynamic-slice_fusion.2
  59.0 1.5 fusion.63
  60.4 3.1 bitcast_dynamic-update-slice_fusion.2
  63.7 1.7 multiply_convert_fusion.2
  68.3 1.5 fusion.63
  69.7 3.1 bitcast_dynamic-update-slice_fusion.2
  73.0 1.7 multiply_convert_fusion.2
  74.7 1.1 constant_dynamic-slice_fusion.2
  77.5 1.5 fusion.63
  79.0 3.0 bitcast_dynamic-update-slice_fusion.2
  82.2 13.2 %scatter_custom_fusion.1 = f32[24,512]{1,0:T(8,128)S(1)} fusion(s32[2048]{0:T(1024)S(1)} %bitcast.107, f32[2048,512]{1,0:T(8,128)} %bitcast.109, f32[]{:T(128)} %constant.77.clone.1), kind=kCustom, calls=%fused_computation.45 | custom fusion | flops 1048576 | bytes 49664 | tf_op jit(solution)/shard_map/scatter-add | solution.py:136
  95.5 1.9 collective-permute-start.2
  97.4 2.4 collective-permute-start.3
  99.9 3.8 %reduce_sum.94 = f32[512,512]{1,0:T(8,128)} reduce(f32[4,512,512]{2,1,0:T(8,128)} %get-tuple-element.73, f32[]{:T(128)} %constant.77.clone.1), dimensions={0}, to_apply=%region_13.14 | reduce | flops 786432 | bytes 5242884 | tf_op jit(solution)/shard_map/reduce_sum | solution.py:133
  103.7 13.7 %scatter_custom_fusion = f32[512,512]{1,0:T(8,128)S(1)} fusion(s32[2048]{0:T(1024)} %bitcast.108, f32[2048,512]{1,0:T(8,128)} %bitcast.110, f32[]{:T(128)} %constant.77.clone.1), kind=kCustom, calls=%fused_computation.35 | custom fusion | flops 1048576 | bytes 1049088 | tf_op jit(solution)/shard_map/scatter-add | solution.py:142
  118.2 3.5 %all-to-all-start = ((bf16[4,128,512]{2,1,0:T(8,128)(2,1)}), bf16[4,128,512]{2,1,0:T(8,128)(2,1)S(1)}, u32[]{:S(2)}, u32[]{:S(2)}) async-start(bf16[4,128,512]{2,1,0:T(8,128)(2,1)} %bitcast.17), calls=%async_computation | async-start | bytes 1048576 | tf_op jit(solution)/shard_map/all_to_all | solution.py:37
  123.0 8.4 %all-to-all-done = bf16[4,128,512]{2,1,0:T(8,128)(2,1)S(1)} async-done(((bf16[4,128,512]{2,1,0:T(8,128)(2,1)}), bf16[4,128,512]{2,1,0:T(8,128)(2,1)S(1)}, u32[]{:S(2)}, u32[]{:S(2)}) %all-to-all-start) | async-done | bytes 524320 | tf_op jit(solution)/shard_map/all_to_all | solution.py:37
  132.5 1.2 fusion.14
  133.7 185.9 %all-reduce.2 = (bf16[512,512]{0,1:T(8,128)(2,1)S(1)}, bf16[512,512]{1,0:T(8,128)(2,1)}, bf16[512,512]{1,0:T(8,128)(2,1)}, f32[512]{0:T(512)}, f32[512]{0:T(512)}) all-reduce(f32[512,512]{0,1:T(8,128)S(1)} %convolution_bitcast_fusion.1, f32[512,512]{1,0:T(8,128)S(1)} %fusion.14, ...), channel_id=1, replica_groups=mesh['space'=128,'level'=4] {'space','level'}, use_global_device_ids=true, to_apply=%region_11.12 | all-reduce | flops 787456 | bytes 4726784 | tf_op jit(solution)/shard_map/psum | solution.py:153
  (89 shorter events, 16.2 us)
Async XLA Ops:
  0.6 17.1 %copy-start = (bf16[512,512]{1,0:T(8,128)(2,1)S(1)}, bf16[512,512]{1,0:T(8,128)(2,1)}, u32[]{:S(2)}) copy-start(bf16[512,512]{1,0:T(8,128)(2,1)} %param.15) | copy-start | bytes 1572868
  1.9 33.9 %collective-permute-start.1 = (bf16[8,512]{1,0:T(8,128)(2,1)S(1)}, bf16[8,512]{1,0:T(8,128)(2,1)S(1)}, u32[]{:S(2)}, u32[]{:S(2)}) collective-permute-start(bf16[8,512]{1,0:T(8,128)(2,1)S(1)} %convolution_convert_fusion), channel_id=1, source_target_pairs={{4,0},{8,4},{12,8},{16,12},{20,16},{24,20},{28,24},{32,28},{36,32}... | collective-permute-start | bytes 24584 | tf_op jit(solution)/shard_map/ppermute | solution.py:17
  10.7 25.1 %collective-permute-start = (bf16[8,512]{1,0:T(8,128)(2,1)S(1)}, bf16[8,512]{1,0:T(8,128)(2,1)S(1)}, u32[]{:S(2)}, u32[]{:S(2)}) collective-permute-start(bf16[8,512]{1,0:T(8,128)(2,1)S(1)} %convolution_convert_fusion), channel_id=1, source_target_pairs={{0,4},{4,8},{8,12},{12,16},{16,20},{20,24},{24,28},{28,32},{32,36}... | collective-permute-start | bytes 24584 | tf_op jit(solution)/shard_map/ppermute | solution.py:15
  35.8 9.2 %copy-start.1 = (bf16[512,512]{1,0:T(8,128)(2,1)S(1)}, bf16[512,512]{1,0:T(8,128)(2,1)}, u32[]{:S(2)}) copy-start(bf16[512,512]{1,0:T(8,128)(2,1)} %param.18) | copy-start | bytes 1572868
  35.8 9.2 %copy-start.4 = (f32[512]{0:T(512)S(1)}, f32[512]{0:T(512)}, u32[]{:S(2)}) copy-start(f32[512]{0:T(512)} %param.20) | copy-start | bytes 6148
  35.8 9.2 %copy-start.5 = (f32[512]{0:T(512)S(1)}, f32[512]{0:T(512)}, u32[]{:S(2)}) copy-start(f32[512]{0:T(512)} %param.19) | copy-start | bytes 6148
  95.5 26.3 %collective-permute-start.2 = (f32[8,512]{1,0:T(8,128)S(1)}, f32[8,512]{1,0:T(8,128)S(1)}, u32[]{:S(2)}, u32[]{:S(2)}) collective-permute-start(f32[8,512]{1,0:T(8,128)S(1)} %get-tuple-element.173), channel_id=1, source_target_pairs={{0,4},{4,8},{8,12},{12,16},{16,20},{20,24},{24,28},{28,32},{32,36}... | collective-permute-start | bytes 49160 | tf_op jit(solution)/shard_map/ppermute | solution.py:27
  97.4 24.4 %collective-permute-start.3 = (f32[8,512]{1,0:T(8,128)S(1)}, f32[8,512]{1,0:T(8,128)S(1)}, u32[]{:S(2)}, u32[]{:S(2)}) collective-permute-start(f32[8,512]{1,0:T(8,128)S(1)} %get-tuple-element.174), channel_id=1, source_target_pairs={{4,0},{8,4},{12,8},{16,12},{20,16},{24,20},{28,24},{32,28},{36,32}... | collective-permute-start | bytes 49160 | tf_op jit(solution)/shard_map/ppermute | solution.py:27
  99.8 21.9 %copy-start.6 = (bf16[1,8,512]{2,1,0:T(8,128)(2,1)S(1)}, bf16[1,8,512]{2,1,0:T(8,128)(2,1)}, u32[]{:S(2)}) copy-start(bf16[1,8,512]{2,1,0:T(8,128)(2,1)} %param.14) | copy-start | bytes 24580
  99.8 22.3 %copy-start.2 = (bf16[512,512]{1,0:T(8,128)(2,1)S(1)}, bf16[512,512]{1,0:T(8,128)(2,1)}, u32[]{:S(2)}) copy-start(bf16[512,512]{1,0:T(8,128)(2,1)} %param.16) | copy-start | bytes 1572868
  103.7 27.8 %copy-start.3 = (bf16[512,512]{1,0:T(8,128)(2,1)S(1)}, bf16[512,512]{1,0:T(8,128)(2,1)}, u32[]{:S(2)}) copy-start(bf16[512,512]{1,0:T(8,128)(2,1)} %param.17) | copy-start | bytes 1572868
  118.2 13.2 %all-to-all-start = ((bf16[4,128,512]{2,1,0:T(8,128)(2,1)}), bf16[4,128,512]{2,1,0:T(8,128)(2,1)S(1)}, u32[]{:S(2)}, u32[]{:S(2)}) async-start(bf16[4,128,512]{2,1,0:T(8,128)(2,1)} %bitcast.17), calls=%async_computation | async-start | bytes 1048576 | tf_op jit(solution)/shard_map/all_to_all | solution.py:37
where the time goes:
time: 322 us; the launch traced here: 321 us
  blocking collectives  186 us (58%)
  other arithmetic  45.8 us (14%)
  local copies, waits for them, and re-layouts  34.4 us (11%)
  matrix products  26.5 us (8%)
  starting transfers between devices  18.5 us (6%)
  waiting for transfers between devices  8.44 us (3%)
    psum x1, blocking collectives, body(): lax.psum((wsend_part, wrecv_part, output_weight_piece, bias_piece, gain_p...  186 us
    scatter-add x1, other arithmetic, body(): jax.ops.segment_sum(preactivation_gradient, receiver_index, num_segments=...  13.7 us
    scatter-add x1, other arithmetic, body(): jax.ops.segment_sum(preactivation_gradient, table_row, num_segments=3 * m...  13.2 us
    dot_general x4, matrix products, edge_reverse_step(): jnp.dot(d_outer_b, output_weight.T, preferred_element_type=jnp.float32)  12.2 us
    gather x1, local copies, waits for them, and re-layouts, body(): sending_rows = table[table_row]  9.18 us
    gather x1, local copies, waits for them, and re-layouts, body(): grid_output_cotangent[receiver_index].reshape(blocks, block, width)  9.15 us
    gather x1, local copies, waits for them, and re-layouts, body(): projected_receiver[receiver_index].reshape(blocks, block, width)  8.9 us
    ppermute x1, starting transfers between devices, with_halo(): lax.ppermute(head, axis, [((i + 1) % count, i) for i in range(ends)])  8.75 us
  transfers between devices with their start and end apart: 5, of which 1 were waited for; matrix products, arithmetic and copies ran while one was open for 13% of the time, Pallas kernels for 0%

commit v1 on v0

v1 whole, which is shorter than its diff:
```python
import jax
import jax.numpy as jnp
from jax import lax
from jax.experimental import pallas as pl
from jax.experimental.pallas import tpu as pltpu
from jax.sharding import PartitionSpec as P

F32 = jnp.float32
BF16 = jnp.bfloat16
NT = (((1,), (1,)), ((), ()))
TN = (((0,), (0,)), ((), ()))
PAD = 128
BLOCK = 256


def mm(a, b, dims=(((1,), (0,)), ((), ()))):
    return lax.dot_general(a, b, dims, preferred_element_type=F32)


def edge_kernel(
    grid_ref,
    cot_ref,
    win_ref,
    w_send_ref,
    w_recv_ref,
    w_out_ref,
    bias_ref,
    gain_ref,
    recv_ref,
    row_ref,
    g_ref,
    vec_ref,
    level_ref,
    table_grad_ref,
    table,
    pick,
    pick_t,
    hid,
    dact,
    douter,
    dpre,
):
    grid_rows, width = grid_ref.shape
    slots = recv_ref.shape[1]
    window = win_ref.shape[0]
    table[0:grid_rows] = mm(grid_ref[...], w_recv_ref[...]).astype(BF16)
    table[grid_rows : grid_rows + PAD] = jnp.zeros((PAD, width), BF16)
    table[grid_rows : grid_rows + window] = mm(win_ref[...], w_send_ref[...]).astype(BF16)

    def build(i, carry):
        at = pl.multiple_of(i * 128, 128)
        recv = recv_ref[:, pl.ds(at, 128)]
        row = row_ref[:, pl.ds(at, 128)]
        recv_b = jnp.broadcast_to(recv, (128, 128))
        row_b = jnp.broadcast_to(row, (128, 128))
        recv_c = recv_b.T
        row_c = row_b.T
        lane = lax.broadcasted_iota(jnp.int32, (128, 128), 1)
        sub = lax.broadcasted_iota(jnp.int32, (128, 128), 0)
        for k in range(grid_rows // 128):
            pick[pl.ds(at, 128), k * 128 : (k + 1) * 128] = (lane + k * 128 == recv_c).astype(
                F32
            ).astype(BF16)
            pick_t[k * 128 : (k + 1) * 128, pl.ds(at, 128)] = (sub + k * 128 == recv_b).astype(
                F32
            ).astype(BF16)
        pick[pl.ds(at, 128), grid_rows : grid_rows + PAD] = (lane == row_c).astype(F32).astype(BF16)
        pick_t[grid_rows : grid_rows + PAD, pl.ds(at, 128)] = (
            (sub == row_b).astype(F32).astype(BF16)
        )
        return carry

    lax.fori_loop(0, slots // 128, build, 0)
    bias = bias_ref[...]
    gain = gain_ref[...]
    scale = 1.0 / width

    def forward(i, acc):
        at = pl.multiple_of(i * BLOCK, BLOCK)
        rows = pl.ds(at, BLOCK)
        preact = mm(pick[rows, :], table[...]) + bias
        sig = jax.nn.sigmoid(preact)
        hidden = preact * sig
        hidden_b = hidden.astype(BF16)
        hid[rows, :] = hidden_b
        dact[rows, :] = sig + hidden * (1.0 - sig)
        outer = mm(hidden_b, w_out_ref[...])
        upstream = mm(pick[rows, 0:grid_rows], cot_ref[...])
        center = outer - jnp.sum(outer, axis=-1, keepdims=True) * scale
        inv = lax.rsqrt(jnp.sum(center * center, axis=-1, keepdims=True) * scale + 1e-05)
        normed = center * inv
        scaled = upstream * gain
        m1 = jnp.sum(scaled, axis=-1, keepdims=True) * scale
        m2 = jnp.sum(scaled * normed, axis=-1, keepdims=True) * scale
        douter[rows, :] = (inv * (scaled - m1 - normed * m2)).astype(BF16)
        part = upstream * normed
        return acc + jnp.sum(part.reshape(BLOCK // 8, 8, width), axis=0)

    gain_acc = lax.fori_loop(0, slots // BLOCK, forward, jnp.zeros((8, width), F32))
    g_ref[2 * width : 3 * width] = mm(hid[...], douter[...], TN).astype(g_ref.dtype)

    def backward(i, acc):
        at = pl.multiple_of(i * BLOCK, BLOCK)
        rows = pl.ds(at, BLOCK)
        d_pre = mm(douter[rows, :], w_out_ref[...], NT) * dact[rows, :]
        dpre[rows, :] = d_pre.astype(BF16)
        return acc + jnp.sum(d_pre.reshape(BLOCK // 8, 8, width), axis=0)

    bias_acc = lax.fori_loop(0, slots // BLOCK, backward, jnp.zeros((8, width), F32))
    vec_ref[0:1] = jnp.sum(bias_acc, axis=0, keepdims=True)
    vec_ref[1:2] = jnp.sum(gain_acc, axis=0, keepdims=True)
    sums = mm(pick_t[...], dpre[...])
    level = sums[0:grid_rows].astype(BF16)
    level_ref[...] = level
    grads = sums[grid_rows : grid_rows + window]
    table_grad_ref[...] = grads
    g_ref[width : 2 * width] = mm(grid_ref[...], level, TN).astype(g_ref.dtype)
    g_ref[0:width] = mm(win_ref[...], grads.astype(BF16), TN).astype(g_ref.dtype)


def edge_call(grid, cot, win, w_send, w_recv, w_out, bias, gain, recv, row, g_dtype=F32):
    grid_rows, width = grid.shape
    slots = recv.shape[1]
    vmem = pl.BlockSpec(memory_space=pltpu.VMEM)
    flops = 2 * slots * width * width * 7
    return pl.pallas_call(
        edge_kernel,
        out_shape=(
            jax.ShapeDtypeStruct((3 * width, width), g_dtype),
            jax.ShapeDtypeStruct((2, width), F32),
            jax.ShapeDtypeStruct((grid_rows, width), BF16),
            jax.ShapeDtypeStruct((win.shape[0], width), F32),
        ),
        in_specs=[vmem] * 10,
        out_specs=(vmem,) * 4,
        scratch_shapes=[
            pltpu.VMEM((grid_rows + PAD, width), BF16),
            pltpu.VMEM((slots, grid_rows + PAD), BF16),
            pltpu.VMEM((grid_rows + PAD, slots), BF16),
            pltpu.VMEM((slots, width), BF16),
            pltpu.VMEM((slots, width), F32),
            pltpu.VMEM((slots, width), BF16),
            pltpu.VMEM((slots, width), BF16),
        ],
        compiler_params=pltpu.CompilerParams(vmem_limit_bytes=48 * 1024 * 1024),
        cost_estimate=pl.CostEstimate(flops=flops, bytes_accessed=8 << 20, transcendentals=0),
    )(grid, cot, win, w_send, w_recv, w_out, bias, gain, recv, row)


def rows_of(edge_sender, edge_receiver, edge_live, mesh_rows):
    sender = edge_sender[0:1]
    band = lax.axis_index("space")
    target = band + sender // mesh_rows - 1
    inside = (target >= 0) & (target < lax.axis_size("space"))
    row = jnp.where(inside, sender, mesh_rows + sender % mesh_rows)
    recv = jnp.where(edge_live[0:1] > 0, edge_receiver[0:1], -1)
    return recv, row


def from_behind(block, axis, distance):
    devices = range(lax.axis_size(axis))
    route = [(i - distance, i) for i in devices if i - distance in devices]
    return lax.ppermute(block, axis, route)


def body(
    grid_latent,
    mesh_latent,
    grid_output_cotangent,
    w_send,
    w_recv,
    output_weight,
    hidden_layer_bias,
    output_norm_gain,
    edge_sender,
    edge_receiver,
    edge_live,
):
    width = grid_latent.shape[1]
    grid_rows = grid_latent.shape[0]
    mesh_rows = mesh_latent.shape[1]
    own = mesh_latent[0]
    win = jnp.concatenate(
        [
            from_behind(own, "space", 1),
            own,
            from_behind(own, "space", -1),
            jnp.zeros((mesh_rows, width), BF16),
        ],
        axis=0,
    )
    recv, row = rows_of(edge_sender, edge_receiver, edge_live, mesh_rows)
    g, vec, level, grads = edge_call(
        grid_latent,
        grid_output_cotangent,
        win,
        w_send,
        w_recv,
        output_weight,
        hidden_layer_bias[None],
        output_norm_gain[None],
        recv,
        row,
        BF16,
    )
    below = grads[:mesh_rows]
    above = grads[2 * mesh_rows : 3 * mesh_rows]
    mesh_acc = (
        grads[mesh_rows : 2 * mesh_rows]
        + from_behind(above, "space", 1)
        + from_behind(below, "space", -1)
    )
    levels = lax.axis_size("level")
    tiles = lax.all_to_all(level.reshape(levels, -1, width), "level", 0, 0, tiled=True)
    grid_sum = jnp.sum(tiles.astype(F32), axis=0).astype(BF16)
    d_mesh = jnp.dot(mesh_acc.astype(BF16), w_send.T, preferred_element_type=F32)[None]
    d_grid = jnp.dot(grid_sum, w_recv.T, preferred_element_type=F32)
    total, vec = lax.psum((g.astype(F32), vec), ("space", "level"))
    total = total.astype(BF16)
    return (
        d_grid,
        d_mesh,
        total[:width],
        total[width : 2 * width],
        total[2 * width :],
        vec[0],
        vec[1],
    )


def solution(mesh):
    return jax.shard_map(
        body,
        mesh=mesh,
        in_specs=(
            P("space", None),
            P("level", "space", None),
            P("space", None),
            P(),
            P(),
            P(),
            P(),
            P(),
            P("level", "space"),
            P("level", "space"),
            P("level", "space"),
        ),
        out_specs=(P(("space", "level"), None), P("level", "space", None), P(), P(), P(), P(), P()),
        check_vma=False,
    )
```

time: 322 us -> 546 us (1.70)
  waiting for transfers between devices: 8.44 us -> 370 us
  blocking collectives: 186 us -> 111 us
  other arithmetic: 45.8 us -> 1.66 us
  matrix products: 26.5 us -> 1.87 us
  local copies, waits for them, and re-layouts: 34.4 us -> 9.78 us
  Pallas kernels: 0 us -> 17.1 us
  between operations: 0.9 us -> 14.1 us
    psum x0 -> x1, waiting for transfers between devices: none -> 368 us  [body(): total, vec = lax.psum((g.astype(F32), vec), ('space', 'level'))]
    psum x1, blocking collectives: 186 us -> 111 us  [body(): total, vec = lax.psum((g.astype(F32), vec), ('space', 'level'))]
    gather x3 -> x0, local copies, waits for them, and re-layouts: 27.2 us -> none  [the longest x1 9.18 us: body(): sending_rows = table[table_row]]
    scatter-add x2 -> x0, other arithmetic: 26.9 us -> none  [the longest x1 13.7 us: body(): jax.ops.segment_sum(preactivation_gradient, receiver_index, num_segments=...]
    dot_general x18 -> x2, matrix products: 26.5 us -> 1.87 us  [the longest x1 1.01 us: body(): d_grid = jnp.dot(grid_sum, w_recv.T, preferred_element_type=F32)]
    pallas_call x0 -> x1, Pallas kernels: none -> 17.1 us  [edge_call(): pl.pallas_call(edge_kernel, out_shape=(jax.ShapeDtypeStruct((3 * width, w...]
    ppermute x2 -> x4, starting transfers between devices: 4.32 us -> 16.4 us  [from_behind(): return lax.ppermute(block, axis, route)]
    ppermute x2 -> x0, starting transfers between devices: 10.7 us -> none  [the longest x1 8.75 us: with_halo(): lax.ppermute(head, axis, [((i + 1) % count, i) for i in range(ends)])]
  transfers between devices with their start and end apart: 5 -> 6, of which waited for: 1 -> 2; matrix products, arithmetic and copies ran while one was open for 13% -> 1% of each run, Pallas kernels for 0% -> 0%
where the time goes in v1:
time: 546 us; the launch traced here: 545 us
  waiting for transfers between devices  370 us (68%)
  blocking collectives  111 us (20%)
  starting transfers between devices  20.1 us (4%)
  Pallas kernels  17.1 us (3%)
  between operations  14.1 us (3%)
  local copies, waits for them, and re-layouts  9.78 us (2%)
    psum x1, waiting for transfers between devices, body(): total, vec = lax.psum((g.astype(F32), vec), ('space', 'level'))  368 us
    psum x1, blocking collectives, body(): total, vec = lax.psum((g.astype(F32), vec), ('space', 'level'))  111 us
    pallas_call x1, Pallas kernels, edge_call(): pl.pallas_call(edge_kernel, out_shape=(jax.ShapeDtypeStruct((3 * width, w...  17.1 us
    ppermute x4, starting transfers between devices, from_behind(): return lax.ppermute(block, axis, route)  16.4 us
  transfers between devices with their start and end apart: 6, of which 2 were waited for; matrix products, arithmetic and copies ran while one was open for 1% of the time, Pallas kernels for 0%

profile of v1, /device:TPU:1, one launch (start us, length us, event | category | flops | bytes accessed | tf_op | source)
XLA Modules:
  0.0 544.8 jit_solution(6148344837029233145)
XLA Ops:
  7.2 8.7 %collective-permute-start.1 = (bf16[8,512]{1,0:T(8,128)(2,1)}, bf16[8,512]{1,0:T(8,128)(2,1)S(1)}, u32[]{:S(2)}, u32[]{:S(2)}) collective-permute-start(bf16[8,512]{1,0:T(8,128)(2,1)} %bitcast.13), channel_id=1, source_target_pairs={{4,0},{8,4},{12,8},{16,12},{20,16},{24,20},{28,24},{32,28},{36,32}... | collective-permute-start | bytes 24584 | tf_op jit(solution)/shard_map/ppermute | solution.py:163
  15.9 1.9 collective-permute-start
  17.9 0.8 and_select_fusion.1
  18.7 0.1 pad.3.clone
  18.8 0.0 collective-permute-done.1
  18.8 0.4 collective-permute-done
  19.2 0.8 maximum_maximum_fusion.win_ref
  20.0 1.0 copy-done
  21.0 1.0 copy-done.2
  22.1 1.0 copy-done.4
  23.1 1.0 copy-done.5
  24.1 1.0 copy-done.6
  25.2 0.7 copy-done.7
  25.9 0.7 copy-done.8
  26.5 17.1 %shard_map.162 = (bf16[1536,512]{1,0:T(8,128)(2,1)}, f32[2,512]{1,0:T(2,128)S(1)}, bf16[512,512]{1,0:T(8,128)(2,1)}, f32[32,512]{1,0:T(8,128)S(1)}) custom-call(bf16[512,512]{1,0:T(8,128)(2,1)S(1)} %copy-done.4, bf16[512,512]{1,0:T(8,128)(2,1)S(1)} %copy-done.5, bf16[32,512]{1,0:T(8,128)(2,1)S(1)} %maximum_maximum_fusion.win_ref, ...), custom_call_target="tpu_custom_call" | custom-call | flops 7516192768 | bytes 8388608 | tf_op jit(solution)/shard_map/pallas_call | solution.py:126
  43.6 3.6 all-to-all-start
  47.3 0.0 copy-start.1
  47.3 0.0 all-reduce.2.cloned.1.call-start
  47.3 0.7 all-reduce.2.cloned.1.call-update
  48.0 2.1 collective-permute-start.3
  50.1 3.7 collective-permute-start.2
  53.8 110.7 %psum.15 = f32[2,512]{1,0:T(2,128)S(1)} all-reduce(f32[2,512]{1,0:T(2,128)S(1)} %get-tuple-element.14), channel_id=1, replica_groups=mesh['space'=128,'level'=4] {'space','level'}, use_global_device_ids=true, to_apply=%region_2.3 | all-reduce | flops 1024 | bytes 8192 | tf_op jit(solution)/shard_map/psum | solution.py:218
  164.5 0.6 fusion.3
  165.1 0.0 collective-permute-done.3
  165.1 0.0 collective-permute-done.2
  165.1 0.9 convolution_bitcast_fusion
  165.9 0.0 all-to-all-done
  165.9 0.1 reduce_sum.12
  166.0 0.0 copy-done.1
  166.0 1.0 fusion.4
  167.0 368.4 %all-reduce.2.cloned.1.call-done = bf16[1536,512]{1,0:T(8,128)(2,1)} async-done(((bf16[1536,512]{1,0:T(8,128)(2,1)}), bf16[1536,512]{1,0:T(8,128)(2,1)}) %all-reduce.2.cloned.1.call-update) | async-done | bytes 1572880 | tf_op jit(solution)/shard_map/psum | solution.py:218
  535.4 2.5 fusion.1
  (11 shorter events, 0.0 us)
Async XLA Ops:
  7.2 11.6 %collective-permute-start.1 = (bf16[8,512]{1,0:T(8,128)(2,1)}, bf16[8,512]{1,0:T(8,128)(2,1)S(1)}, u32[]{:S(2)}, u32[]{:S(2)}) collective-permute-start(bf16[8,512]{1,0:T(8,128)(2,1)} %bitcast.13), channel_id=1, source_target_pairs={{4,0},{8,4},{12,8},{16,12},{20,16},{24,20},{28,24},{32,28},{36,32}... | collective-permute-start | bytes 24584 | tf_op jit(solution)/shard_map/ppermute | solution.py:163
  15.9 3.3 collective-permute-start
  20.0 1.0 copy-start
  21.0 1.0 copy-start.2
  22.1 1.0 copy-start.4
  23.1 1.0 copy-start.5
  24.1 1.0 copy-start.6
  25.2 0.7 copy-start.7
  25.9 0.7 copy-start.8
  43.6 121.4 %copy-start.3 = (bf16[512,512]{1,0:T(8,128)(2,1)S(1)}, bf16[512,512]{1,0:T(8,128)(2,1)}, u32[]{:S(2)}) copy-start(bf16[512,512]{1,0:T(8,128)(2,1)} %w_send_ref.1) | copy-start | bytes 1572868
  43.6 122.3 %all-to-all-start = ((bf16[4,128,512]{2,1,0:T(8,128)(2,1)}), bf16[4,128,512]{2,1,0:T(8,128)(2,1)S(1)}, u32[]{:S(2)}, u32[]{:S(2)}) async-start(bf16[4,128,512]{2,1,0:T(8,128)(2,1)} %bitcast.3), calls=%async_computation | async-start | bytes 1048576 | tf_op jit(solution)/shard_map/all_to_all | solution.py:214
  47.3 118.8 %copy-start.1 = (bf16[512,512]{1,0:T(8,128)(2,1)S(1)}, bf16[512,512]{1,0:T(8,128)(2,1)}, u32[]{:S(2)}) copy-start(bf16[512,512]{1,0:T(8,128)(2,1)} %w_recv_ref.1) | copy-start | bytes 1572868
  47.3 488.2 %all-reduce.2.cloned.1.call-start = ((), (), s32[]{:S(2)}) async-start(), calls=%async_computation.1 | async-start | bytes 3145728 | tf_op jit(solution)/shard_map/psum | solution.py:218
  48.0 117.0 %collective-permute-start.3 = (f32[8,512]{1,0:T(8,128)S(1)}, f32[8,512]{1,0:T(8,128)S(1)}, u32[]{:S(2)}, u32[]{:S(2)}) collective-permute-start(f32[8,512]{1,0:T(8,128)S(1)} %get-tuple-element.19), channel_id=1, source_target_pairs={{4,0},{8,4},{12,8},{16,12},{20,16},{24,20},{28,24},{32,28},{36,32}... | collective-permute-start | bytes 49160 | tf_op jit(solution)/shard_map/ppermute | solution.py:163
  50.1 115.0 %collective-permute-start.2 = (f32[8,512]{1,0:T(8,128)S(1)}, f32[8,512]{1,0:T(8,128)S(1)}, u32[]{:S(2)}, u32[]{:S(2)}) collective-permute-start(f32[8,512]{1,0:T(8,128)S(1)} %get-tuple-element.18), channel_id=1, source_target_pairs={{0,4},{4,8},{8,12},{12,16},{16,20},{20,24},{24,28},{28,32},{32,36}... | collective-permute-start | bytes 49160 | tf_op jit(solution)/shard_map/ppermute | solution.py:163
Sparse Core Ops, SparseCore 0:
  53.4 481.9 all-reduce.1

commit v2 on v1

--- a/solution.py
+++ b/solution.py
@@ -145,6 +145,381 @@
         compiler_params=pltpu.CompilerParams(vmem_limit_bytes=48 * 1024 * 1024),
         cost_estimate=pl.CostEstimate(flops=flops, bytes_accessed=8 << 20, transcendentals=0),
     )(grid, cot, win, w_send, w_recv, w_out, bias, gain, recv, row)
+
+
+MESH = pl.DeviceIdType.MESH
+DEPTH = 16
+NEAR = 4
+CHUNKS = ((2, "yx"), (1, "xy"), (0, "yx"))
+
+
+class Ring:
+    def __init__(self):
+        space = lax.axis_index("space")
+        self.count = lax.axis_size("space")
+        self.x = lax.axis_index("level")
+        self.nx = lax.axis_size("level")
+        self.ny = self.count // (2 * DEPTH)
+        self.space = space
+        self.core = lax.rem(space, 2)
+        z = lax.rem(space // 2, DEPTH)
+        self.y = space // (2 * DEPTH)
+        self.near = lax.rem(z, NEAR)
+        self.far = z // NEAR
+
+    def at(self, core=None, y=None, near=None, far=None, x=None):
+        core = self.core if core is None else core
+        y = self.y if y is None else y
+        near = self.near if near is None else near
+        far = self.far if far is None else far
+        x = self.x if x is None else x
+        return {"space": ((y * DEPTH) + far * NEAR + near) * 2 + core, "level": x}
+
+    def peers(self, axis):
+        me, n = {
+            "core": (self.core, 2),
+            "y": (self.y, self.ny),
+            "x": (self.x, self.nx),
+            "near": (self.near, NEAR),
+            "far": (self.far, DEPTH // NEAR),
+        }[axis]
+        out = []
+        for d in range(1, n):
+            to = lax.rem(me + d, n)
+            out.append((d, to, self.at(**{axis: to})))
+        return me, n, out
+
+    def beside(self, step):
+        return {"space": lax.rem(self.space + step + self.count, self.count), "level": self.x}
+
+
+class Copies:
+    def __init__(self, send_sem, recv_sem):
+        self.send_sem, self.recv_sem = send_sem, recv_sem
+        self.used = 0
+        self.all = []
+
+    def start(self, src, dst, device):
+        k = self.used
+        self.used += 1
+        copy = pltpu.make_async_remote_copy(
+            src_ref=src,
+            dst_ref=dst,
+            send_sem=self.send_sem.at[k],
+            recv_sem=self.recv_sem.at[k],
+            device_id=device,
+            device_id_type=MESH,
+        )
+        copy.start()
+        self.all.append(copy)
+        return copy
+
+    def finish(self):
+        for copy in self.all:
+            copy.wait_send()
+
+
+def span(start, size, step):
+    return pl.ds(pl.multiple_of(start, step), size)
+
+
+class Reduce:
+    def __init__(self, ring, copies, index, order, g_ref, out_ref, bufs):
+        self.ring, self.copies = ring, copies
+        self.order = order
+        self.g, self.out = g_ref, out_ref
+        self.core_buf, self.acc1, self.buf1, self.acc2, self.buf2, self.acc3, self.buf3, self.buf4 = bufs
+        self.width = g_ref.shape[1]
+        rows = self.width
+        self.rows = rows
+        self.n1 = rows // 2
+        self.n2 = self.n1 // 4
+        self.n3 = self.n2 // 4
+        self.base = index * rows
+        self.b1, self.b2, self.b3 = index * self.n1, index * self.n2, index * self.n3
+        self.cols = self.width // NEAR
+
+    def wait(self):
+        for copy in self.flight:
+            copy.wait_recv()
+
+    def mine(self, level, a1=None, a2=None):
+        r = self.ring
+        at = self.base + r.core * self.n1
+        if level >= 1:
+            at = at + (getattr(r, self.order[0]) if a1 is None else a1) * self.n2
+        if level >= 2:
+            at = at + (getattr(r, self.order[1]) if a2 is None else a2) * self.n3
+        return span(at, (self.n1, self.n2, self.n3)[level], 16)
+
+    def s0(self):
+        r = self.ring
+        _, _, peers = r.peers("core")
+        ((_, other, device),) = peers
+        src = self.g.at[span(self.base + other * self.n1, self.n1, 16)]
+        self.flight = [self.copies.start(src, self.core_buf.at[pl.ds(self.b1, self.n1)], device)]
+
+    def s1(self):
+        self.wait()
+        mine = self.g[self.mine(0), :].astype(F32)
+        here = pl.ds(self.b1, self.n1)
+        self.acc1[here] = (mine + self.core_buf[here].astype(F32)).astype(BF16)
+        _, _, peers = self.ring.peers(self.order[0])
+        self.flight = []
+        for d, to, device in peers:
+            src = self.acc1.at[span(self.b1 + to * self.n2, self.n2, 16)]
+            dst = self.buf1.at[d - 1, pl.ds(self.b2, self.n2)]
+            self.flight.append(self.copies.start(src, dst, device))
+
+    def s2(self):
+        self.wait()
+        me, n, _ = self.ring.peers(self.order[0])
+        total = self.acc1[span(self.b1 + me * self.n2, self.n2, 16), :].astype(F32)
+        here = pl.ds(self.b2, self.n2)
+        for d in range(n - 1):
+            total = total + self.buf1[d, here].astype(F32)
+        self.acc2[here] = total.astype(BF16)
+        _, _, peers = self.ring.peers(self.order[1])
+        self.flight = []
+        for d, to, device in peers:
+            src = self.acc2.at[span(self.b2 + to * self.n3, self.n3, 16)]
+            dst = self.buf2.at[d - 1, pl.ds(self.b3, self.n3)]
+            self.flight.append(self.copies.start(src, dst, device))
+
+    def s3(self):
+        self.wait()
+        me, n, _ = self.ring.peers(self.order[1])
+        total = self.acc2[span(self.b2 + me * self.n3, self.n3, 16), :].astype(F32)
+        here = pl.ds(self.b3, self.n3)
+        for d in range(n - 1):
+            total = total + self.buf2[d, here].astype(F32)
+        self.acc3[here] = total.astype(BF16)
+        _, _, peers = self.ring.peers("near")
+        self.flight = []
+        for d, to, device in peers:
+            src = self.acc3.at[here, span(to * self.cols, self.cols, 128)]
+            dst = self.buf3.at[d - 1, here]
+            self.flight.append(self.copies.start(src, dst, device))
+
+    def s4(self):
+        self.wait()
+        me, n, _ = self.ring.peers("near")
+        here = pl.ds(self.b3, self.n3)
+        total = self.acc3[here, span(me * self.cols, self.cols, 128)].astype(F32)
+        for d in range(n - 1):
+            total = total + self.buf3[d, here].astype(F32)
+        far, _, peers = self.ring.peers("far")
+        self.buf4[far, here] = total.astype(BF16)
+        self.flight = []
+        for _, _, device in peers:
+            slot = self.buf4.at[far, here]
+            self.flight.append(self.copies.start(slot, slot, device))
+
+    def s5(self):
+        self.wait()
+        here = pl.ds(self.b3, self.n3)
+        _, n, _ = self.ring.peers("far")
+        total = self.buf4[0, here].astype(F32)
+        for k in range(1, n):
+            total = total + self.buf4[k, here].astype(F32)
+        me, _, peers = self.ring.peers("near")
+        rows, cols = self.mine(2), span(me * self.cols, self.cols, 128)
+        self.out[rows, cols] = total.astype(BF16)
+        self.flight = []
+        for _, _, device in peers:
+            part = self.out.at[rows, cols]
+            self.flight.append(self.copies.start(part, part, device))
+
+    def spread(self, axis, level):
+        self.wait()
+        _, _, peers = self.ring.peers(axis)
+        part = self.out.at[self.mine(level)]
+        self.flight = [self.copies.start(part, part, device) for _, _, device in peers]
+
+    def s6(self):
+        self.spread(self.order[1], 2)
+
+    def s7(self):
+        self.spread(self.order[0], 1)
+
+    def s8(self):
+        self.spread("core", 0)
+
+    def s9(self):
+        self.wait()
+
+
+class Vector:
+    AXES = ("core", "y", "x", "near", "far")
+
+    def __init__(self, ring, copies, buf):
+        self.ring, self.copies, self.buf = ring, copies, buf
+        self.step = 0
+
+    def start(self, value):
+        me, n, peers = self.ring.peers(self.AXES[self.step])
+        self.buf[self.step, me] = value
+        slot = self.buf.at[self.step, me]
+        self.flight = [self.copies.start(slot, slot, device) for _, _, device in peers]
+        self.n = n
+
+    def total(self):
+        for copy in self.flight:
+            copy.wait_recv()
+        total = self.buf[self.step, 0]
+        for k in range(1, self.n):
+            total = total + self.buf[self.step, k]
+        self.step += 1
+        return total
+
+    def next(self):
+        self.start(self.total())
+
+
+def greet(ring):
+    barrier = pltpu.get_barrier_semaphore()
+    count = 0
+    for axis in ("far", "near", "y", "x", "core"):
+        for _, _, device in ring.peers(axis)[2]:
+            pl.semaphore_signal(barrier, inc=1, device_id=device, device_id_type=MESH)
+            count += 1
+    outer = ring.beside(2 * ring.core - 1)
+    pl.semaphore_signal(barrier, inc=1, device_id=outer, device_id_type=MESH)
+    return barrier, count + 1
+
+
+def comm_kernel(
+    g_ref,
+    vec_ref,
+    level_ref,
+    grads_ref,
+    w_send_ref,
+    w_recv_ref,
+    out_ref,
+    vec_out_ref,
+    d_grid_ref,
+    d_mesh_ref,
+    out,
+    core_buf,
+    acc1,
+    buf1,
+    acc2,
+    buf2,
+    acc3,
+    buf3,
+    buf4,
+    vec_buf,
+    level_buf,
+    halo_buf,
+    send_sem,
+    recv_sem,
+):
+    ring = Ring()
+    barrier, count = greet(ring)
+    pl.semaphore_wait(barrier, count)
+    copies = Copies(send_sem, recv_sem)
+    bufs = (core_buf, acc1, buf1, acc2, buf2, acc3, buf3, buf4)
+    parts = [Reduce(ring, copies, i, order, g_ref, out, bufs) for i, order in CHUNKS]
+    vec = Vector(ring, copies, vec_buf)
+    for part in parts:
+        part.s0()
+    vec.start(vec_ref[...])
+    for part in parts:
+        part.s1()
+    vec.next()
+    mesh_rows = halo_buf.shape[1]
+    halo = [
+        copies.start(grads_ref.at[pl.ds(2 * mesh_rows, mesh_rows)], halo_buf.at[0], ring.beside(1)),
+        copies.start(grads_ref.at[pl.ds(0, mesh_rows)], halo_buf.at[1], ring.beside(-1)),
+    ]
+    for part in parts:
+        part.s2()
+    vec.next()
+    share = level_buf.shape[1]
+    x, _, x_peers = ring.peers("x")
+    levels = []
+    for d, to, device in x_peers:
+        src = level_ref.at[span(to * share, share, 16)]
+        levels.append(copies.start(src, level_buf.at[d - 1], device))
+    for part in parts:
+        part.s3()
+    vec.next()
+    for part in parts:
+        part.s4()
+    vec.next()
+    for copy in halo:
+        copy.wait_recv()
+    mesh_sum = grads_ref[mesh_rows : 2 * mesh_rows] + halo_buf[0] + halo_buf[1]
+    d_mesh_ref[...] = mm(mesh_sum.astype(BF16), w_send_ref[...], NT)
+    for copy in levels:
+        copy.wait_recv()
+    grid_sum = level_ref[span(x * share, share, 16), :].astype(F32)
+    for d in range(len(levels)):
+        grid_sum = grid_sum + level_buf[d].astype(F32)
+    d_grid_ref[...] = mm(grid_sum.astype(BF16), w_recv_ref[...], NT)
+    for part in parts:
+        part.s5()
+    vec_out_ref[...] = vec.total()
+    for part in parts:
+        part.s6()
+    for part in parts:
+        part.s7()
+    for part in parts:
+        part.s8()
+    for part in parts:
+        part.s9()
+    out_ref[...] = out[...]
+    copies.finish()
+
+
+def comm_scratch(width, grid_rows, mesh_rows, nx, ny):
+    rows = 3 * width
+    n1 = rows // 2
+    n2 = n1 // 4
+    n3 = n2 // 4
+    cols = width // NEAR
+    far = DEPTH // NEAR
+    copies = 3 * (1 + 1 + 4 * (nx - 1 + ny - 1)) + 3 * 3 * (NEAR - 1) + 3 * (far - 1)
+    copies = 160
+    return [
+        pltpu.VMEM((rows, width), BF16),
+        pltpu.VMEM((n1, width), BF16),
+        pltpu.VMEM((n1, width), BF16),
+        pltpu.VMEM((3, n2, width), BF16),
+        pltpu.VMEM((n2, width), BF16),
+        pltpu.VMEM((3, n3, width), BF16),
+        pltpu.VMEM((n3, width), BF16),
+        pltpu.VMEM((NEAR - 1, n3, cols), BF16),
+        pltpu.VMEM((far, n3, cols), BF16),
+        pltpu.VMEM((5, 4, 8, 2 * width // 8), F32),
+        pltpu.VMEM((nx - 1, grid_rows // nx, width), BF16),
+        pltpu.VMEM((2, mesh_rows, width), F32),
+        pltpu.SemaphoreType.DMA((copies,)),
+        pltpu.SemaphoreType.DMA((copies,)),
+    ]
+
+
+def comm_call(g, vec, level, grads, w_send, w_recv, mesh_rows):
+    width = g.shape[1]
+    grid_rows = level.shape[0]
+    nx = lax.axis_size("level")
+    ny = lax.axis_size("space") // (2 * DEPTH)
+    vmem = pl.BlockSpec(memory_space=pltpu.VMEM)
+    return pl.pallas_call(
+        comm_kernel,
+        out_shape=(
+            jax.ShapeDtypeStruct(g.shape, BF16),
+            jax.ShapeDtypeStruct(vec.shape, F32),
+            jax.ShapeDtypeStruct((grid_rows // nx, width), F32),
+            jax.ShapeDtypeStruct((mesh_rows, width), F32),
+        ),
+        in_specs=[vmem] * 6,
+        out_specs=(vmem,) * 4,
+        scratch_shapes=comm_scratch(width, grid_rows, mesh_rows, nx, ny),
+        compiler_params=pltpu.CompilerParams(
+            vmem_limit_bytes=32 * 1024 * 1024, collective_id=0, has_side_effects=True
+        ),
+    )(g, vec, level, grads, w_send, w_recv)
 
 
 def rows_of(edge_sender, edge_receiver, edge_live, mesh_rows):
@@ -203,23 +578,13 @@
         row,
         BF16,
     )
-    below = grads[:mesh_rows]
-    above = grads[2 * mesh_rows : 3 * mesh_rows]
-    mesh_acc = (
-        grads[mesh_rows : 2 * mesh_rows]
-        + from_behind(above, "space", 1)
-        + from_behind(below, "space", -1)
+    total, vec, d_grid, d_mesh = comm_call(
+        g, vec.reshape(8, 2 * width // 8), level, grads, w_send, w_recv, mesh_rows
     )
-    levels = lax.axis_size("level")
-    tiles = lax.all_to_all(level.reshape(levels, -1, width), "level", 0, 0, tiled=True)
-    grid_sum = jnp.sum(tiles.astype(F32), axis=0).astype(BF16)
-    d_mesh = jnp.dot(mesh_acc.astype(BF16), w_send.T, preferred_element_type=F32)[None]
-    d_grid = jnp.dot(grid_sum, w_recv.T, preferred_element_type=F32)
-    total, vec = lax.psum((g.astype(F32), vec), ("space", "level"))
-    total = total.astype(BF16)
+    vec = vec.reshape(2, width)
     return (
         d_grid,
-        d_mesh,
+        d_mesh[None],
         total[:width],
         total[width : 2 * width],
         total[2 * width :],

time: 546 us -> 93.9 us (0.17)
  waiting for transfers between devices: 370 us -> 0.44 us
  blocking collectives: 111 us -> 0 us
  Pallas kernels: 17.1 us -> 70.2 us
  between operations: 14.1 us -> 0.71 us
  starting transfers between devices: 20.1 us -> 10.7 us
    psum x1 -> x0, waiting for transfers between devices: 368 us -> none  [body(): total, vec = lax.psum((g.astype(F32), vec), ('space', 'level'))]
    psum x1 -> x0, blocking collectives: 111 us -> none  [body(): total, vec = lax.psum((g.astype(F32), vec), ('space', 'level'))]
    pallas_call x0 -> x1, Pallas kernels: none -> 54.3 us  [comm_call(): pl.pallas_call(comm_kernel, out_shape=(jax.ShapeDtypeStruct(g.shape, BF16...]
    ppermute x4 -> x2, starting transfers between devices: 16.4 us -> 10.7 us  [from_behind(): return lax.ppermute(block, axis, route)]
  transfers between devices with their start and end apart: 6 -> 2, of which waited for: 2 -> 1; matrix products, arithmetic and copies ran while one was open for 1% -> 1% of each run, Pallas kernels for 0% -> 0%
where the time goes in v2:
time: 93.9 us; the launch traced here: 93.4 us
  Pallas kernels  70.2 us (75%)
  starting transfers between devices  10.7 us (11%)
  local copies, waits for them, and re-layouts  9.73 us (10%)
  other arithmetic  1.58 us (2%)
    pallas_call x1, Pallas kernels, comm_call(): pl.pallas_call(comm_kernel, out_shape=(jax.ShapeDtypeStruct(g.shape, BF16...  54.3 us
    pallas_call x1, Pallas kernels, edge_call(): pl.pallas_call(edge_kernel, out_shape=(jax.ShapeDtypeStruct((3 * width, w...  16 us
    ppermute x2, starting transfers between devices, from_behind(): return lax.ppermute(block, axis, route)  10.7 us
    unnamed x20, local copies, waits for them, and re-layouts  7.88 us
  transfers between devices with their start and end apart: 2, of which 1 were waited for; matrix products, arithmetic and copies ran while one was open for 1% of the time, Pallas kernels for 0%

profile of v2, /device:TPU:1, one launch (start us, length us, event | category | flops | bytes accessed | tf_op | source)
XLA Modules:
  0.0 93.4 jit_solution(16647855649959563784)
XLA Ops:
  0.6 8.7 %collective-permute-start.1 = (bf16[8,512]{1,0:T(8,128)(2,1)}, bf16[8,512]{1,0:T(8,128)(2,1)S(1)}, u32[]{:S(2)}, u32[]{:S(2)}) collective-permute-start(bf16[8,512]{1,0:T(8,128)(2,1)} %bitcast.11), channel_id=1, source_target_pairs={{4,0},{8,4},{12,8},{16,12},{20,16},{24,20},{28,24},{32,28},{36,32}... | collective-permute-start | bytes 24584 | tf_op jit(solution)/shard_map/ppermute | solution.py:538
  9.4 1.9 %collective-permute-start = (bf16[8,512]{1,0:T(8,128)(2,1)}, bf16[8,512]{1,0:T(8,128)(2,1)S(1)}, u32[]{:S(2)}, u32[]{:S(2)}) collective-permute-start(bf16[8,512]{1,0:T(8,128)(2,1)} %bitcast.12), channel_id=1, source_target_pairs={{0,4},{4,8},{8,12},{12,16},{16,20},{20,24},{24,28},{28,32},{32,36}... | collective-permute-start | bytes 24584 | tf_op jit(solution)/shard_map/ppermute | solution.py:538
  11.3 0.8 and_select_fusion.1
  12.1 0.1 pad.3.clone
  12.2 0.0 collective-permute-done.1
  12.2 0.4 collective-permute-done
  12.7 0.8 maximum_maximum_fusion.win_ref
  13.4 0.0 copy-start
  13.4 1.0 %copy-done = bf16[512,512]{1,0:T(8,128)(2,1)S(1)} copy-done((bf16[512,512]{1,0:T(8,128)(2,1)S(1)}, bf16[512,512]{1,0:T(8,128)(2,1)}, u32[]{:S(2)}) %copy-start) | copy-done | bytes 524312
  14.5 0.0 copy-start.2
  14.5 1.0 %copy-done.2 = bf16[512,512]{1,0:T(8,128)(2,1)S(1)} copy-done((bf16[512,512]{1,0:T(8,128)(2,1)S(1)}, bf16[512,512]{1,0:T(8,128)(2,1)}, u32[]{:S(2)}) %copy-start.2) | copy-done | bytes 524312
  15.5 0.0 copy-start.4
  15.5 1.0 %copy-done.4 = bf16[512,512]{1,0:T(8,128)(2,1)S(1)} copy-done((bf16[512,512]{1,0:T(8,128)(2,1)S(1)}, bf16[512,512]{1,0:T(8,128)(2,1)}, u32[]{:S(2)}) %copy-start.4) | copy-done | bytes 524312
  16.6 0.0 copy-start.5
  16.6 1.0 %copy-done.5 = bf16[512,512]{1,0:T(8,128)(2,1)S(1)} copy-done((bf16[512,512]{1,0:T(8,128)(2,1)S(1)}, bf16[512,512]{1,0:T(8,128)(2,1)}, u32[]{:S(2)}) %copy-start.5) | copy-done | bytes 524312
  17.6 0.0 copy-start.6
  17.6 1.0 %copy-done.6 = bf16[512,512]{1,0:T(8,128)(2,1)S(1)} copy-done((bf16[512,512]{1,0:T(8,128)(2,1)S(1)}, bf16[512,512]{1,0:T(8,128)(2,1)}, u32[]{:S(2)}) %copy-start.6) | copy-done | bytes 524312
  18.7 0.0 copy-start.7
  18.7 0.7 copy-done.7
  19.3 0.0 copy-start.8
  19.3 0.7 copy-done.8
  20.0 0.0 copy-start.1
  20.0 0.0 copy-start.3
  20.0 16.0 %shard_map.162 = (bf16[1536,512]{1,0:T(8,128)(2,1)S(1)}, f32[2,512]{1,0:T(2,128)S(1)}, bf16[512,512]{1,0:T(8,128)(2,1)S(1)}, f32[32,512]{1,0:T(8,128)S(1)}) custom-call(bf16[512,512]{1,0:T(8,128)(2,1)S(1)} %copy-done.4, bf16[512,512]{1,0:T(8,128)(2,1)S(1)} %copy-done.5, bf16[32,512]{1,0:T(8,128)(2,1)S(1)} %maximum_maximum_fusion.win_ref, ...), custom_call_target="tpu_custom_call" | custom-call | flops 7516192768 | bytes 8388608 | tf_op jit(solution)/shard_map/pallas_call | solution.py:126
  36.0 0.0 copy-done.1
  36.0 0.0 copy-done.3
  36.0 54.3 %shard_map.163 = (bf16[1536,512]{1,0:T(8,128)(2,1)S(1)}, f32[8,128]{1,0:T(8,128)S(1)}, f32[128,512]{1,0:T(8,128)S(1)}, f32[8,512]{1,0:T(8,128)S(1)}) custom-call(bf16[1536,512]{1,0:T(8,128)(2,1)S(1)} %get-tuple-element.15.g_ref, f32[8,128]{1,0:T(8,128)S(1)} %reshape.22.vec_ref, bf16[512,512]{1,0:T(8,128)(2,1)S(1)} %get-tuple-element.17.level_ref, ...), custom_call_target="tpu_custom_call" | custom-call | tf_op jit(solution)/shard_map/pallas_call | solution.py:508
  90.3 0.6 slice_bitcast_fusion
  90.9 1.2 %fusion.1 = (bf16[512,512]{1,0:T(8,128)(2,1)}, bf16[512,512]{1,0:T(8,128)(2,1)}, bf16[512,512]{1,0:T(8,128)(2,1)}) fusion(bf16[1536,512]{1,0:T(8,128)(2,1)S(1)} %get-tuple-element.21), kind=kLoop, calls=%fused_computation.11 | loop fusion | bytes 3145728 | tf_op jit(solution)/shard_map/slice | solution.py:590
  92.1 0.7 copy.20
  92.8 0.6 copy.21
  (2 shorter events, 0.0 us)
Async XLA Ops:
  0.6 11.6 %collective-permute-start.1 = (bf16[8,512]{1,0:T(8,128)(2,1)}, bf16[8,512]{1,0:T(8,128)(2,1)S(1)}, u32[]{:S(2)}, u32[]{:S(2)}) collective-permute-start(bf16[8,512]{1,0:T(8,128)(2,1)} %bitcast.11), channel_id=1, source_target_pairs={{4,0},{8,4},{12,8},{16,12},{20,16},{24,20},{28,24},{32,28},{36,32}... | collective-permute-start | bytes 24584 | tf_op jit(solution)/shard_map/ppermute | solution.py:538
  9.4 3.3 %collective-permute-start = (bf16[8,512]{1,0:T(8,128)(2,1)}, bf16[8,512]{1,0:T(8,128)(2,1)S(1)}, u32[]{:S(2)}, u32[]{:S(2)}) collective-permute-start(bf16[8,512]{1,0:T(8,128)(2,1)} %bitcast.12), channel_id=1, source_target_pairs={{0,4},{4,8},{8,12},{12,16},{16,20},{20,24},{24,28},{28,32},{32,36}... | collective-permute-start | bytes 24584 | tf_op jit(solution)/shard_map/ppermute | solution.py:538
  13.4 1.0 %copy-start = (bf16[512,512]{1,0:T(8,128)(2,1)S(1)}, bf16[512,512]{1,0:T(8,128)(2,1)}, u32[]{:S(2)}) copy-start(bf16[512,512]{1,0:T(8,128)(2,1)} %w_send_ref.3) | copy-start | bytes 1572868
  14.5 1.0 %copy-start.2 = (bf16[512,512]{1,0:T(8,128)(2,1)S(1)}, bf16[512,512]{1,0:T(8,128)(2,1)}, u32[]{:S(2)}) copy-start(bf16[512,512]{1,0:T(8,128)(2,1)} %w_recv_ref.3) | copy-start | bytes 1572868
  15.5 1.0 %copy-start.4 = (bf16[512,512]{1,0:T(8,128)(2,1)S(1)}, bf16[512,512]{1,0:T(8,128)(2,1)}, u32[]{:S(2)}) copy-start(bf16[512,512]{1,0:T(8,128)(2,1)} %grid_ref.1) | copy-start | bytes 1572868
  16.6 1.0 %copy-start.5 = (bf16[512,512]{1,0:T(8,128)(2,1)S(1)}, bf16[512,512]{1,0:T(8,128)(2,1)}, u32[]{:S(2)}) copy-start(bf16[512,512]{1,0:T(8,128)(2,1)} %cot_ref.1) | copy-start | bytes 1572868
  17.6 1.0 %copy-start.6 = (bf16[512,512]{1,0:T(8,128)(2,1)S(1)}, bf16[512,512]{1,0:T(8,128)(2,1)}, u32[]{:S(2)}) copy-start(bf16[512,512]{1,0:T(8,128)(2,1)} %w_out_ref.1) | copy-start | bytes 1572868
  18.7 0.7 copy-start.7
  19.3 0.7 copy-start.8
  20.0 16.0 %copy-start.1 = (bf16[512,512]{1,0:T(8,128)(2,1)S(1)}, bf16[512,512]{1,0:T(8,128)(2,1)}, u32[]{:S(2)}) copy-start(bf16[512,512]{1,0:T(8,128)(2,1)} %w_send_ref.3) | copy-start | bytes 1572868
  20.0 16.0 %copy-start.3 = (bf16[512,512]{1,0:T(8,128)(2,1)S(1)}, bf16[512,512]{1,0:T(8,128)(2,1)}, u32[]{:S(2)}) copy-start(bf16[512,512]{1,0:T(8,128)(2,1)} %w_recv_ref.3) | copy-start | bytes 1572868

commit v3 on v2

v3 whole, which is shorter than its diff:
```python
import jax
import jax.numpy as jnp
from jax import lax
from jax.experimental import pallas as pl
from jax.experimental.pallas import tpu as pltpu
from jax.sharding import PartitionSpec as P

F32 = jnp.float32
BF16 = jnp.bfloat16
NT = (((1,), (1,)), ((), ()))
TN = (((0,), (0,)), ((), ()))
PAD = 128
BLOCK = 256
PREP_VMEM = 24 << 20
MAIN_VMEM = 40 << 20


def mm(a, b, dims=(((1,), (0,)), ((), ()))):
    return lax.dot_general(a, b, dims, preferred_element_type=F32)


MESH = pl.DeviceIdType.MESH
DEPTH = 16
NEAR = 4
EARLY = ((2, "yx"),)
LATE = ((1, "xy"), (0, "yx"))


class Ring:
    def __init__(self):
        space = lax.axis_index("space")
        self.count = lax.axis_size("space")
        self.x = lax.axis_index("level")
        self.nx = lax.axis_size("level")
        self.ny = self.count // (2 * DEPTH)
        self.space = space
        self.core = lax.rem(space, 2)
        z = lax.rem(space // 2, DEPTH)
        self.y = space // (2 * DEPTH)
        self.near = lax.rem(z, NEAR)
        self.far = z // NEAR

    def at(self, core=None, y=None, near=None, far=None, x=None):
        core = self.core if core is None else core
        y = self.y if y is None else y
        near = self.near if near is None else near
        far = self.far if far is None else far
        x = self.x if x is None else x
        return {"space": ((y * DEPTH) + far * NEAR + near) * 2 + core, "level": x}

    def peers(self, axis):
        me, n = {
            "core": (self.core, 2),
            "y": (self.y, self.ny),
            "x": (self.x, self.nx),
            "near": (self.near, NEAR),
            "far": (self.far, DEPTH // NEAR),
        }[axis]
        out = []
        for d in range(1, n):
            to = lax.rem(me + d, n)
            out.append((d, to, self.at(**{axis: to})))
        return me, n, out

    def beside(self, step):
        return {"space": lax.rem(self.space + step + self.count, self.count), "level": self.x}


class Copies:
    def __init__(self, send_sem, recv_sem):
        self.send_sem, self.recv_sem = send_sem, recv_sem
        self.used = 0
        self.all = []

    def start(self, src, dst, device):
        k = self.used
        self.used += 1
        copy = pltpu.make_async_remote_copy(
            src_ref=src,
            dst_ref=dst,
            send_sem=self.send_sem.at[k],
            recv_sem=self.recv_sem.at[k],
            device_id=device,
            device_id_type=MESH,
        )
        copy.start()
        self.all.append(copy)
        return copy

    def finish(self):
        for copy in self.all:
            copy.wait_send()


def span(start, size, step):
    return pl.ds(pl.multiple_of(start, step), size)


class Reduce:
    def __init__(self, ring, copies, index, order, g_ref, out_ref, bufs):
        self.ring, self.copies = ring, copies
        self.order = order
        self.g, self.out = g_ref, out_ref
        self.core_buf, self.acc1, self.buf1, self.acc2, self.buf2, self.acc3, self.buf3, self.buf4 = bufs
        self.width = g_ref.shape[1]
        rows = self.width
        self.rows = rows
        self.n1 = rows // 2
        self.n2 = self.n1 // 4
        self.n3 = self.n2 // 4
        self.base = index * rows
        self.b1, self.b2, self.b3 = index * self.n1, index * self.n2, index * self.n3
        self.cols = self.width // NEAR

    def wait(self):
        for copy in self.flight:
            copy.wait_recv()

    def mine(self, level, a1=None, a2=None):
        r = self.ring
        at = self.base + r.core * self.n1
        if level >= 1:
            at = at + (getattr(r, self.order[0]) if a1 is None else a1) * self.n2
        if level >= 2:
            at = at + (getattr(r, self.order[1]) if a2 is None else a2) * self.n3
        return span(at, (self.n1, self.n2, self.n3)[level], 16)

    def s0(self):
        r = self.ring
        _, _, peers = r.peers("core")
        ((_, other, device),) = peers
        src = self.g.at[span(self.base + other * self.n1, self.n1, 16)]
        self.flight = [self.copies.start(src, self.core_buf.at[pl.ds(self.b1, self.n1)], device)]

    def s1(self):
        self.wait()
        mine = self.g[self.mine(0), :].astype(F32)
        here = pl.ds(self.b1, self.n1)
        self.acc1[here] = (mine + self.core_buf[here].astype(F32)).astype(BF16)
        _, _, peers = self.ring.peers(self.order[0])
        self.flight = []
        for d, to, device in peers:
            src = self.acc1.at[span(self.b1 + to * self.n2, self.n2, 16)]
            dst = self.buf1.at[d - 1, pl.ds(self.b2, self.n2)]
            self.flight.append(self.copies.start(src, dst, device))

    def s2(self):
        self.wait()
        me, n, _ = self.ring.peers(self.order[0])
        total = self.acc1[span(self.b1 + me * self.n2, self.n2, 16), :].astype(F32)
        here = pl.ds(self.b2, self.n2)
        for d in range(n - 1):
            total = total + self.buf1[d, here].astype(F32)
        self.acc2[here] = total.astype(BF16)
        _, _, peers = self.ring.peers(self.order[1])
        self.flight = []
        for d, to, device in peers:
            src = self.acc2.at[span(self.b2 + to * self.n3, self.n3, 16)]
            dst = self.buf2.at[d - 1, pl.ds(self.b3, self.n3)]
            self.flight.append(self.copies.start(src, dst, device))

    def s3(self):
        self.wait()
        me, n, _ = self.ring.peers(self.order[1])
        total = self.acc2[span(self.b2 + me * self.n3, self.n3, 16), :].astype(F32)
        here = pl.ds(self.b3, self.n3)
        for d in range(n - 1):
            total = total + self.buf2[d, here].astype(F32)
        self.acc3[here] = total.astype(BF16)
        _, _, peers = self.ring.peers("near")
        self.flight = []
        for d, to, device in peers:
            src = self.acc3.at[here, span(to * self.cols, self.cols, 128)]
            dst = self.buf3.at[d - 1, here]
            self.flight.append(self.copies.start(src, dst, device))

    def s4(self):
        self.wait()
        me, n, _ = self.ring.peers("near")
        here = pl.ds(self.b3, self.n3)
        total = self.acc3[here, span(me * self.cols, self.cols, 128)].astype(F32)
        for d in range(n - 1):
            total = total + self.buf3[d, here].astype(F32)
        far, _, peers = self.ring.peers("far")
        self.buf4[far, here] = total.astype(BF16)
        self.flight = []
        for _, _, device in peers:
            slot = self.buf4.at[far, here]
            self.flight.append(self.copies.start(slot, slot, device))

    def s5(self):
        self.wait()
        here = pl.ds(self.b3, self.n3)
        _, n, _ = self.ring.peers("far")
        total = self.buf4[0, here].astype(F32)
        for k in range(1, n):
            total = total + self.buf4[k, here].astype(F32)
        me, _, peers = self.ring.peers("near")
        rows, cols = self.mine(2), span(me * self.cols, self.cols, 128)
        self.out[rows, cols] = total.astype(BF16)
        self.flight = []
        for _, _, device in peers:
            part = self.out.at[rows, cols]
            self.flight.append(self.copies.start(part, part, device))

    def spread(self, axis, level):
        self.wait()
        _, _, peers = self.ring.peers(axis)
        part = self.out.at[self.mine(level)]
        self.flight = [self.copies.start(part, part, device) for _, _, device in peers]

    def s6(self):
        self.spread(self.order[1], 2)

    def s7(self):
        self.spread(self.order[0], 1)

    def s8(self):
        self.spread("core", 0)

    def s9(self):
        self.wait()


class Vector:
    AXES = ("core", "y", "x", "near", "far")

    def __init__(self, ring, copies, buf):
        self.ring, self.copies, self.buf = ring, copies, buf
        self.step = 0

    def start(self, value):
        me, n, peers = self.ring.peers(self.AXES[self.step])
        self.buf[self.step, me] = value
        slot = self.buf.at[self.step, me]
        self.flight = [self.copies.start(slot, slot, device) for _, _, device in peers]
        self.n = n

    def total(self):
        for copy in self.flight:
            copy.wait_recv()
        total = self.buf[self.step, 0]
        for k in range(1, self.n):
            total = total + self.buf[self.step, k]
        self.step += 1
        return total

    def next(self):
        self.start(self.total())


def greet(ring):
    barrier = pltpu.get_barrier_semaphore()
    count = 0
    for axis in ("far", "near", "y", "x", "core"):
        for _, _, device in ring.peers(axis)[2]:
            pl.semaphore_signal(barrier, inc=1, device_id=device, device_id_type=MESH)
            count += 1
    outer = ring.beside(2 * ring.core - 1)
    pl.semaphore_signal(barrier, inc=1, device_id=outer, device_id_type=MESH)
    return barrier, count + 1


def prep_kernel(
    grid_hbm,
    cot_hbm,
    own_hbm,
    w_send_hbm,
    w_recv_hbm,
    w_out_hbm,
    bias_hbm,
    gain_hbm,
    sender_hbm,
    recv_hbm,
    live_hbm,
    table,
    pick,
    pick_t,
    win,
    grid,
    cot,
    w_send,
    w_recv,
    w_out,
    bias,
    gain,
    index,
    mesh_buf,
    local_sem,
    send_sem,
    recv_sem,
):
    ring = Ring()
    barrier = pltpu.get_barrier_semaphore()
    for step in (-1, 1):
        pl.semaphore_signal(barrier, inc=1, device_id=ring.beside(step), device_id_type=MESH)
    loads = []
    for src, dst in (
        (own_hbm, mesh_buf.at[1]),
        (sender_hbm, index.at[0]),
        (recv_hbm, index.at[1]),
        (live_hbm, index.at[2]),
        (grid_hbm, grid),
        (w_recv_hbm, w_recv),
        (w_send_hbm, w_send),
        (w_out_hbm, w_out),
        (cot_hbm, cot),
        (bias_hbm, bias),
        (gain_hbm, gain),
    ):
        copy = pltpu.make_async_copy(src, dst, local_sem.at[len(loads)])
        copy.start()
        loads.append(copy)
    grid_rows, width = grid.shape
    slots = index.shape[2]
    mesh_rows = mesh_buf.shape[1]
    for copy in loads[:4]:
        copy.wait()
    pl.semaphore_wait(barrier, 2)
    copies = Copies(send_sem, recv_sem)
    halo = [
        copies.start(mesh_buf.at[1], mesh_buf.at[0], ring.beside(1)),
        copies.start(mesh_buf.at[1], mesh_buf.at[2], ring.beside(-1)),
    ]

    def build(i, carry):
        at = pl.multiple_of(i * 128, 128)
        sender = index[0, :, pl.ds(at, 128)]
        target = ring.space + (sender >> 3) - 1
        inside = (target >= 0) & (target < ring.count)
        row = jnp.where(inside, sender, mesh_rows + (sender & (mesh_rows - 1)))
        recv = jnp.where(index[2, :, pl.ds(at, 128)] > 0, index[1, :, pl.ds(at, 128)], -1)
        recv_b = jnp.broadcast_to(recv, (128, 128))
        row_b = jnp.broadcast_to(row, (128, 128))
        recv_c = recv_b.T
        row_c = row_b.T
        lane = lax.broadcasted_iota(jnp.int32, (128, 128), 1)
        sub = lax.broadcasted_iota(jnp.int32, (128, 128), 0)
        for k in range(grid_rows // 128):
            pick[pl.ds(at, 128), k * 128 : (k + 1) * 128] = (lane + k * 128 == recv_c).astype(
                F32
            ).astype(BF16)
            pick_t[k * 128 : (k + 1) * 128, pl.ds(at, 128)] = (sub + k * 128 == recv_b).astype(
                F32
            ).astype(BF16)
        pick[pl.ds(at, 128), grid_rows : grid_rows + PAD] = (lane == row_c).astype(F32).astype(BF16)
        pick_t[grid_rows : grid_rows + PAD, pl.ds(at, 128)] = (
            (sub == row_b).astype(F32).astype(BF16)
        )
        return carry

    lax.fori_loop(0, slots // 128, build, 0)
    loads[4].wait()
    loads[5].wait()
    table[0:grid_rows] = mm(grid[...], w_recv[...]).astype(BF16)
    table[grid_rows : grid_rows + PAD] = jnp.zeros((PAD, width), BF16)
    loads[6].wait()
    for copy in halo:
        copy.wait_recv()
    for k in range(3):
        win[k * mesh_rows : (k + 1) * mesh_rows] = mesh_buf[k]
    win[3 * mesh_rows : 4 * mesh_rows] = jnp.zeros((mesh_rows, width), BF16)
    window = win.shape[0]
    table[grid_rows : grid_rows + window] = mm(win[...], w_send[...]).astype(BF16)
    for copy in loads[7:]:
        copy.wait()
    copies.finish()


def prep_call(grid, cot, own, w_send, w_recv, w_out, bias, gain, sender, recv, live):
    grid_rows, width = grid.shape
    slots = recv.shape[1]
    mesh_rows = own.shape[0]
    vmem = pl.BlockSpec(memory_space=pltpu.VMEM)
    anywhere = pl.BlockSpec(memory_space=pltpu.HBM)
    square = jax.ShapeDtypeStruct((width, width), BF16)
    outs = (
        jax.ShapeDtypeStruct((grid_rows + PAD, width), BF16),
        jax.ShapeDtypeStruct((slots, grid_rows + PAD), BF16),
        jax.ShapeDtypeStruct((grid_rows + PAD, slots), BF16),
        jax.ShapeDtypeStruct((4 * mesh_rows, width), BF16),
        jax.ShapeDtypeStruct(grid.shape, BF16),
        jax.ShapeDtypeStruct(cot.shape, BF16),
        square,
        square,
        square,
        jax.ShapeDtypeStruct(bias.shape, F32),
        jax.ShapeDtypeStruct(gain.shape, F32),
    )
    return pl.pallas_call(
        prep_kernel,
        out_shape=outs,
        in_specs=[anywhere] * 11,
        out_specs=(vmem,) * len(outs),
        scratch_shapes=[
            pltpu.VMEM((3, 1, slots), jnp.int32),
            pltpu.VMEM((3, mesh_rows, width), BF16),
            pltpu.SemaphoreType.DMA((11,)),
            pltpu.SemaphoreType.DMA((2,)),
            pltpu.SemaphoreType.DMA((2,)),
        ],
        compiler_params=pltpu.CompilerParams(
            vmem_limit_bytes=PREP_VMEM, collective_id=0, has_side_effects=True
        ),
    )(*(pltpu.with_memory_space_constraint(a, pltpu.HBM) for a in (grid, cot, own, w_send, w_recv, w_out, bias, gain, sender, recv, live)))


def comm_scratch(width, grid_rows, mesh_rows, nx, ny):
    rows = 3 * width
    n1 = rows // 2
    n2 = n1 // 4
    n3 = n2 // 4
    cols = width // NEAR
    far = DEPTH // NEAR
    copies = 160
    return [
        pltpu.VMEM((rows, width), BF16),
        pltpu.VMEM((n1, width), BF16),
        pltpu.VMEM((n1, width), BF16),
        pltpu.VMEM((3, n2, width), BF16),
        pltpu.VMEM((n2, width), BF16),
        pltpu.VMEM((3, n3, width), BF16),
        pltpu.VMEM((n3, width), BF16),
        pltpu.VMEM((NEAR - 1, n3, cols), BF16),
        pltpu.VMEM((far, n3, cols), BF16),
        pltpu.VMEM((5, 4, 2, width), F32),
        pltpu.VMEM((nx - 1, grid_rows // nx, width), BF16),
        pltpu.VMEM((2, mesh_rows, width), F32),
        pltpu.SemaphoreType.DMA((copies,)),
        pltpu.SemaphoreType.DMA((copies,)),
    ]


def main_kernel(
    table,
    pick,
    pick_t,
    win_ref,
    grid_ref,
    cot_ref,
    w_send_ref,
    w_recv_ref,
    w_out_ref,
    bias_ref,
    gain_ref,
    out,
    vec_out_ref,
    d_grid_ref,
    d_mesh_ref,
    total,
    g_ref,
    level_ref,
    grads_ref,
    hid,
    dact,
    douter,
    dpre,
    *comm,
):
    *bufs, vec_buf, level_buf, halo_buf, send_sem, recv_sem = comm
    ring = Ring()
    barrier, count = greet(ring)
    grid_rows, width = grid_ref.shape
    slots = pick.shape[0]
    window = win_ref.shape[0]
    mesh_rows = halo_buf.shape[1]
    bias = bias_ref[...]
    gain = gain_ref[...]
    scale = 1.0 / width

    def forward(i, acc):
        at = pl.multiple_of(i * BLOCK, BLOCK)
        rows = pl.ds(at, BLOCK)
        preact = mm(pick[rows, :], table[...]) + bias
        half = 0.5 * preact
        turn = jnp.tanh(half)
        hidden = half + half * turn
        sig = 0.5 + 0.5 * turn
        hidden_b = hidden.astype(BF16)
        hid[rows, :] = hidden_b
        dact[rows, :] = sig + (hidden - hidden * sig)
        outer = mm(hidden_b, w_out_ref[...])
        upstream = mm(pick[rows, 0:grid_rows], cot_ref[...])
        center = outer - jnp.sum(outer, axis=-1, keepdims=True) * scale
        inv = lax.rsqrt(jnp.sum(center * center, axis=-1, keepdims=True) * scale + 1e-05)
        normed = center * inv
        scaled = upstream * gain
        m1 = jnp.sum(scaled, axis=-1, keepdims=True) * scale
        m2 = jnp.sum(scaled * normed, axis=-1, keepdims=True) * scale
        douter[rows, :] = (inv * (scaled - m1 - normed * m2)).astype(BF16)
        part = upstream * normed
        return acc + jnp.sum(part.reshape(BLOCK // 8, 8, width), axis=0)

    gain_acc = lax.fori_loop(0, slots // BLOCK, forward, jnp.zeros((8, width), F32))
    g_ref[2 * width : 3 * width] = mm(hid[...], douter[...], TN).astype(BF16)
    pl.semaphore_wait(barrier, count)
    copies = Copies(send_sem, recv_sem)
    early = [Reduce(ring, copies, i, order, g_ref, total, bufs) for i, order in EARLY]
    late = [Reduce(ring, copies, i, order, g_ref, total, bufs) for i, order in LATE]
    parts = early + late
    for part in early:
        part.s0()

    def backward(i, acc):
        at = pl.multiple_of(i * BLOCK, BLOCK)
        rows = pl.ds(at, BLOCK)
        d_pre = mm(douter[rows, :], w_out_ref[...], NT) * dact[rows, :]
        dpre[rows, :] = d_pre.astype(BF16)
        return acc + jnp.sum(d_pre.reshape(BLOCK // 8, 8, width), axis=0)

    bias_acc = lax.fori_loop(0, slots // BLOCK, backward, jnp.zeros((8, width), F32))
    for part in early:
        part.s1()
    sums = mm(pick_t[...], dpre[...])
    level = sums[0:grid_rows].astype(BF16)
    level_ref[...] = level
    grads = sums[grid_rows : grid_rows + window]
    grads_ref[...] = grads
    g_ref[width : 2 * width] = mm(grid_ref[...], level, TN).astype(BF16)
    g_ref[0:width] = mm(win_ref[...], grads.astype(BF16), TN).astype(BF16)
    for part in late:
        part.s0()
    vec = Vector(ring, copies, vec_buf)
    pair = jnp.concatenate(
        [jnp.sum(bias_acc, axis=0, keepdims=True), jnp.sum(gain_acc, axis=0, keepdims=True)], axis=0
    )
    vec.start(pair)
    for part in late:
        part.s1()
    vec.next()
    halo = [
        copies.start(grads_ref.at[pl.ds(2 * mesh_rows, mesh_rows)], halo_buf.at[0], ring.beside(1)),
        copies.start(grads_ref.at[pl.ds(0, mesh_rows)], halo_buf.at[1], ring.beside(-1)),
    ]
    for part in parts:
        part.s2()
    vec.next()
    share = level_buf.shape[1]
    x, _, x_peers = ring.peers("x")
    levels = []
    for d, to, device in x_peers:
        src = level_ref.at[span(to * share, share, 16)]
        levels.append(copies.start(src, level_buf.at[d - 1], device))
    for part in parts:
        part.s3()
    vec.next()
    for part in parts:
        part.s4()
    vec.next()
    for copy in halo:
        copy.wait_recv()
    mesh_sum = grads_ref[mesh_rows : 2 * mesh_rows] + halo_buf[0] + halo_buf[1]
    d_mesh_ref[...] = mm(mesh_sum.astype(BF16), w_send_ref[...], NT)
    for copy in levels:
        copy.wait_recv()
    grid_sum = level_ref[span(x * share, share, 16), :].astype(F32)
    for d in range(len(levels)):
        grid_sum = grid_sum + level_buf[d].astype(F32)
    d_grid_ref[...] = mm(grid_sum.astype(BF16), w_recv_ref[...], NT)
    for part in parts:
        part.s5()
    vec_out_ref[...] = vec.total()
    for part in parts:
        part.s6()
    for part in parts:
        part.s7()
    for part in parts:
        part.s8()
    for part in parts:
        part.s9()
    out[...] = total[...]
    copies.finish()


def main_call(inputs, mesh_rows):
    grid_rows, width = inputs[4].shape
    slots = inputs[1].shape[0]
    nx = lax.axis_size("level")
    ny = lax.axis_size("space") // (2 * DEPTH)
    vmem = pl.BlockSpec(memory_space=pltpu.VMEM)
    comm = comm_scratch(width, grid_rows, mesh_rows, nx, ny)
    return pl.pallas_call(
        main_kernel,
        out_shape=(
            jax.ShapeDtypeStruct((3 * width, width), BF16),
            jax.ShapeDtypeStruct((2, width), F32),
            jax.ShapeDtypeStruct((grid_rows // nx, width), F32),
            jax.ShapeDtypeStruct((mesh_rows, width), F32),
        ),
        in_specs=[vmem] * len(inputs),
        out_specs=(vmem,) * 4,
        scratch_shapes=[
            comm[0],
            pltpu.VMEM((3 * width, width), BF16),
            pltpu.VMEM((grid_rows, width), BF16),
            pltpu.VMEM((4 * mesh_rows, width), F32),
            pltpu.VMEM((slots, width), BF16),
            pltpu.VMEM((slots, width), F32),
            pltpu.VMEM((slots, width), BF16),
            pltpu.VMEM((slots, width), BF16),
            *comm[1:],
        ],
        compiler_params=pltpu.CompilerParams(
            vmem_limit_bytes=MAIN_VMEM, collective_id=1, has_side_effects=True
        ),
    )(*inputs)


def tail_kernel(total, vec, d_grid, d_mesh, *refs):
    *outs, sem = refs
    width = total.shape[1]
    sources = [
        d_grid,
        d_mesh,
        *(total.at[pl.ds(k * width, width)] for k in range(3)),
        vec.at[pl.ds(0, 1)],
        vec.at[pl.ds(1, 1)],
    ]
    copies = [
        pltpu.make_async_copy(src, dst, sem.at[k]) for k, (src, dst) in enumerate(zip(sources, outs))
    ]
    for copy in copies:
        copy.start()
    for copy in copies:
        copy.wait()


def tail_call(total, vec, d_grid, d_mesh):
    width = total.shape[1]
    vmem = pl.BlockSpec(memory_space=pltpu.VMEM)
    anywhere = pl.BlockSpec(memory_space=pl.ANY)
    square = jax.ShapeDtypeStruct((width, width), BF16)
    line = jax.ShapeDtypeStruct((1, width), F32)
    outs = (
        jax.ShapeDtypeStruct(d_grid.shape, F32),
        jax.ShapeDtypeStruct(d_mesh.shape, F32),
        square,
        square,
        square,
        line,
        line,
    )
    return pl.pallas_call(
        tail_kernel,
        out_shape=outs,
        in_specs=[vmem] * 4,
        out_specs=(anywhere,) * len(outs),
        scratch_shapes=[pltpu.SemaphoreType.DMA((len(outs),))],
        compiler_params=pltpu.CompilerParams(vmem_limit_bytes=1 << 20),
    )(total, vec, d_grid, d_mesh)


def body(
    grid_latent,
    mesh_latent,
    grid_output_cotangent,
    w_send,
    w_recv,
    output_weight,
    hidden_layer_bias,
    output_norm_gain,
    edge_sender,
    edge_receiver,
    edge_live,
):
    inputs = prep_call(
        grid_latent,
        grid_output_cotangent,
        mesh_latent[0],
        w_send,
        w_recv,
        output_weight,
        hidden_layer_bias[None],
        output_norm_gain[None],
        edge_sender,
        edge_receiver,
        edge_live,
    )
    results = main_call(inputs, mesh_latent.shape[1])
    d_grid, d_mesh, d_w_send, d_w_recv, d_w_out, d_bias, d_gain = tail_call(*results)
    return (d_grid, d_mesh[None], d_w_send, d_w_recv, d_w_out, d_bias[0], d_gain[0])


def solution(mesh):
    return jax.shard_map(
        body,
        mesh=mesh,
        in_specs=(
            P("space", None),
            P("level", "space", None),
            P("space", None),
            P(),
            P(),
            P(),
            P(),
            P(),
            P("level", "space"),
            P("level", "space"),
            P("level", "space"),
        ),
        out_specs=(P(("space", "level"), None), P("level", "space", None), P(), P(), P(), P(), P()),
        check_vma=False,
    )
```

time: 93.9 us -> 74.3 us (0.79)
  starting transfers between devices: 10.7 us -> 0 us
  local copies, waits for them, and re-layouts: 9.73 us -> 0 us
  Pallas kernels: 70.2 us -> 73.5 us
  other arithmetic: 1.58 us -> 0 us
    ppermute x2 -> x0, starting transfers between devices: 10.7 us -> none  [from_behind(): return lax.ppermute(block, axis, route)]
    unnamed x20 -> x0, local copies, waits for them, and re-layouts: 7.88 us -> none
    pallas_call x2 -> x3, Pallas kernels: 70.2 us -> 73.5 us  [the longest x1 57.6 us: main_call(): pl.pallas_call(main_kernel, out_shape=(jax.ShapeDtypeStruct((3 * width, w...]
    slice x1 -> x0, local copies, waits for them, and re-layouts: 1.17 us -> none  [body(): total[2 * width:]]
  transfers between devices with their start and end apart: 2 -> 0, of which waited for: 1 -> 0; matrix products, arithmetic and copies ran while one was open for 1% -> 0% of each run, Pallas kernels for 0% -> 0%
where the time goes in v3:
time: 74.3 us; the launch traced here: 74.1 us
  Pallas kernels  73.5 us (99%)
    pallas_call x1, Pallas kernels, main_call(): pl.pallas_call(main_kernel, out_shape=(jax.ShapeDtypeStruct((3 * width, w...  57.6 us
    pallas_call x1, Pallas kernels, prep_call(): pl.pallas_call(prep_kernel, out_shape=outs, in_specs=[anywhere] * 11, out...  14.6 us

profile of v3, /device:TPU:1, one launch (start us, length us, event | category | flops | bytes accessed | tf_op | source)
XLA Modules:
  0.0 74.1 jit_solution(5718545810428798549)
XLA Ops:
  0.6 14.6 %shard_map.162 = (bf16[640,512]{1,0:T(8,128)(2,1)S(1)}, bf16[2048,640]{1,0:T(8,128)(2,1)S(1)}, bf16[640,2048]{1,0:T(8,128)(2,1)S(1)}, bf16[32,512]{1,0:T(8,128)(...) custom-call(bf16[512,512]{1,0:T(8,128)(2,1)} %grid_hbm.1, ...), custom_call_target="tpu_custom_call" | custom-call | tf_op jit(solution)/shard_map/pallas_call | solution.py:390
  15.3 57.6 %shard_map.163 = (bf16[1536,512]{1,0:T(8,128)(2,1)S(1)}, f32[2,512]{1,0:T(2,128)S(1)}, f32[128,512]{1,0:T(8,128)S(1)}, f32[8,512]{1,0:T(8,128)S(1)}) custom-call(bf16[640,512]{1,0:T(8,128)(2,1)S(1)} %get-tuple-element.29.table, bf16[2048,640]{1,0:T(8,128)(2,1)S(1)} %get-tuple-element.30.pick, bf16[640,2048]{1,0:T(8,128)(2,1)S(1)} %get-tuple-element.31.pick_t, ...), custom_call_target="tpu_custom_call" | custom-call | tf_op jit(solution)/shard_map/pallas_call | solution.py:582
  72.8 1.3 %shard_map.164 = (f32[128,512]{1,0:T(8,128)}, f32[8,512]{1,0:T(8,128)}, bf16[512,512]{1,0:T(8,128)(2,1)}, bf16[512,512]{1,0:T(8,128)(2,1)}, bf16[512,512]{1,0:T(...) custom-call(bf16[1536,512]{1,0:T(8,128)(2,1)S(1)} %get-tuple-element.40.total, f32[2,512]{1,0:T(2,128)S(1)} %get-tuple-element.41.vec, ...), custom_call_target="tpu_custom_call" | custom-call | tf_op jit(solution)/shard_map/pallas_call | solution.py:643

commit v4 on v3

--- a/solution.py
+++ b/solution.py
@@ -11,6 +11,7 @@
 TN = (((0,), (0,)), ((), ()))
 PAD = 128
 BLOCK = 256
+STRIP = 16
 PREP_VMEM = 24 << 20
 MAIN_VMEM = 40 << 20
 
@@ -282,8 +283,9 @@
     w_send,
     w_recv,
     w_out,
+    w_back,
+    gain,
     bias,
-    gain,
     index,
     mesh_buf,
     local_sem,
@@ -352,8 +354,11 @@
     lax.fori_loop(0, slots // 128, build, 0)
     loads[4].wait()
     loads[5].wait()
-    table[0:grid_rows] = mm(grid[...], w_recv[...]).astype(BF16)
+    loads[9].wait()
+    table[0:grid_rows] = (0.5 * (mm(grid[...], w_recv[...]) + bias[...])).astype(BF16)
     table[grid_rows : grid_rows + PAD] = jnp.zeros((PAD, width), BF16)
+    loads[7].wait()
+    w_back[...] = (0.5 * w_out[...].astype(F32)).T.astype(BF16)
     loads[6].wait()
     for copy in halo:
         copy.wait_recv()
@@ -361,9 +366,10 @@
         win[k * mesh_rows : (k + 1) * mesh_rows] = mesh_buf[k]
     win[3 * mesh_rows : 4 * mesh_rows] = jnp.zeros((mesh_rows, width), BF16)
     window = win.shape[0]
-    table[grid_rows : grid_rows + window] = mm(win[...], w_send[...]).astype(BF16)
-    for copy in loads[7:]:
-        copy.wait()
+    send = mm(win[...], w_send[...]).astype(BF16)
+    table[grid_rows : grid_rows + window] = (0.5 * send.astype(F32)).astype(BF16)
+    loads[8].wait()
+    loads[10].wait()
     copies.finish()
 
 
@@ -384,7 +390,7 @@
         square,
         square,
         square,
-        jax.ShapeDtypeStruct(bias.shape, F32),
+        square,
         jax.ShapeDtypeStruct(gain.shape, F32),
     )
     return pl.pallas_call(
@@ -393,6 +399,7 @@
         in_specs=[anywhere] * 11,
         out_specs=(vmem,) * len(outs),
         scratch_shapes=[
+            pltpu.VMEM(bias.shape, F32),
             pltpu.VMEM((3, 1, slots), jnp.int32),
             pltpu.VMEM((3, mesh_rows, width), BF16),
             pltpu.SemaphoreType.DMA((11,)),
@@ -441,13 +448,12 @@
     w_send_ref,
     w_recv_ref,
     w_out_ref,
-    bias_ref,
+    w_back_ref,
     gain_ref,
-    out,
+    total,
     vec_out_ref,
     d_grid_ref,
     d_mesh_ref,
-    total,
     g_ref,
     level_ref,
     grads_ref,
@@ -455,8 +461,9 @@
     dact,
     douter,
     dpre,
-    *comm,
+    *rest,
 ):
+    stage, comm = rest[:12], rest[12:]
     *bufs, vec_buf, level_buf, halo_buf, send_sem, recv_sem = comm
     ring = Ring()
     barrier, count = greet(ring)
@@ -464,34 +471,97 @@
     slots = pick.shape[0]
     window = win_ref.shape[0]
     mesh_rows = halo_buf.shape[1]
-    bias = bias_ref[...]
     gain = gain_ref[...]
     scale = 1.0 / width
-
-    def forward(i, acc):
-        at = pl.multiple_of(i * BLOCK, BLOCK)
-        rows = pl.ds(at, BLOCK)
-        preact = mm(pick[rows, :], table[...]) + bias
-        half = 0.5 * preact
-        turn = jnp.tanh(half)
-        hidden = half + half * turn
-        sig = 0.5 + 0.5 * turn
-        hidden_b = hidden.astype(BF16)
-        hid[rows, :] = hidden_b
-        dact[rows, :] = sig + (hidden - hidden * sig)
-        outer = mm(hidden_b, w_out_ref[...])
-        upstream = mm(pick[rows, 0:grid_rows], cot_ref[...])
-        center = outer - jnp.sum(outer, axis=-1, keepdims=True) * scale
-        inv = lax.rsqrt(jnp.sum(center * center, axis=-1, keepdims=True) * scale + 1e-05)
-        normed = center * inv
-        scaled = upstream * gain
-        m1 = jnp.sum(scaled, axis=-1, keepdims=True) * scale
-        m2 = jnp.sum(scaled * normed, axis=-1, keepdims=True) * scale
-        douter[rows, :] = (inv * (scaled - m1 - normed * m2)).astype(BF16)
-        part = upstream * normed
-        return acc + jnp.sum(part.reshape(BLOCK // 8, 8, width), axis=0)
-
-    gain_acc = lax.fori_loop(0, slots // BLOCK, forward, jnp.zeros((8, width), F32))
+    blocks = slots // BLOCK
+    halves, hiddens, outers, ups, douters, backs = (stage[2 * k : 2 * k + 2] for k in range(6))
+
+    def rows_at(i, r=0, size=BLOCK):
+        start = i * BLOCK
+        if not isinstance(i, int):
+            start = pl.multiple_of(start, BLOCK)
+        return pl.ds(start + r, size)
+
+    def gather(i, slot):
+        halves[slot][...] = mm(pick[rows_at(i), :], table[...])
+
+    def activate(i, slot):
+        for r in range(0, BLOCK, STRIP):
+            strip = slice(r, r + STRIP)
+            half = halves[slot][strip, :]
+            turn = jnp.tanh(half)
+            plus = 1.0 + turn
+            hidden = half * plus
+            hidden_b = hidden.astype(BF16)
+            hiddens[slot][strip, :] = hidden_b
+            hid[rows_at(i, r, STRIP), :] = hidden_b
+            dact[rows_at(i, r, STRIP), :] = plus + hidden * (1.0 - turn)
+
+    def project(i, slot):
+        outers[slot][...] = mm(hiddens[slot][...], w_out_ref[...])
+        ups[slot][...] = mm(pick[rows_at(i), 0:grid_rows], cot_ref[...])
+
+    def normalize(i, slot, acc):
+        for r in range(0, BLOCK, STRIP):
+            strip = slice(r, r + STRIP)
+            outer = outers[slot][strip, :]
+            upstream = ups[slot][strip, :]
+            center = outer - jnp.sum(outer, axis=-1, keepdims=True) * scale
+            inv = lax.rsqrt(jnp.sum(center * center, axis=-1, keepdims=True) * scale + 1e-05)
+            normed = center * inv
+            scaled = upstream * gain
+            part = upstream * normed
+            m1 = jnp.sum(scaled, axis=-1, keepdims=True) * scale
+            m2 = jnp.sum(part * gain, axis=-1, keepdims=True) * scale
+            d_outer = (inv * (scaled - m1 - normed * m2)).astype(BF16)
+            douters[slot][strip, :] = d_outer
+            douter[rows_at(i, r, STRIP), :] = d_outer
+            acc = acc + jnp.sum(part.reshape(STRIP // 8, 8, width), axis=0)
+        return acc
+
+    def back(i, slot):
+        backs[slot][...] = mm(douters[slot][...], w_back_ref[...])
+
+    def differentiate(i, slot, acc):
+        for r in range(0, BLOCK, STRIP):
+            d_pre = backs[slot][r : r + STRIP, :] * dact[rows_at(i, r, STRIP), :]
+            dpre[rows_at(i, r, STRIP), :] = d_pre.astype(BF16)
+            acc = acc + jnp.sum(d_pre.reshape(STRIP // 8, 8, width), axis=0)
+        return acc
+
+    def tick(t, parity, accs):
+        bias_acc, gain_acc = accs
+
+        def on(lag):
+            return not isinstance(t, int) or 0 <= t - lag < blocks
+
+        if on(5):
+            bias_acc = differentiate(t - 5, (parity + 1) % 2, bias_acc)
+        if on(4):
+            back(t - 4, parity)
+        if on(3):
+            gain_acc = normalize(t - 3, (parity + 1) % 2, gain_acc)
+        if on(2):
+            project(t - 2, parity)
+        if on(1):
+            activate(t - 1, (parity + 1) % 2)
+        if on(0):
+            gather(t, parity)
+        return bias_acc, gain_acc
+
+    zero = jnp.zeros((8, width), F32)
+    accs = (zero, zero)
+    for t in range(6):
+        accs = tick(t, t % 2, accs)
+
+    def pair(j, accs):
+        t = 6 + 2 * j
+        return tick(t + 1, 1, tick(t, 0, accs))
+
+    accs = lax.fori_loop(0, (blocks - 6) // 2, pair, accs)
+    for t in range(blocks, blocks + 5):
+        accs = tick(t, t % 2, accs)
+    bias_acc, gain_acc = accs
     g_ref[2 * width : 3 * width] = mm(hid[...], douter[...], TN).astype(BF16)
     pl.semaphore_wait(barrier, count)
     copies = Copies(send_sem, recv_sem)
@@ -501,17 +571,9 @@
     for part in early:
         part.s0()
 
-    def backward(i, acc):
-        at = pl.multiple_of(i * BLOCK, BLOCK)
-        rows = pl.ds(at, BLOCK)
-        d_pre = mm(douter[rows, :], w_out_ref[...], NT) * dact[rows, :]
-        dpre[rows, :] = d_pre.astype(BF16)
-        return acc + jnp.sum(d_pre.reshape(BLOCK // 8, 8, width), axis=0)
-
-    bias_acc = lax.fori_loop(0, slots // BLOCK, backward, jnp.zeros((8, width), F32))
+    sums = mm(pick_t[...], dpre[...])
     for part in early:
         part.s1()
-    sums = mm(pick_t[...], dpre[...])
     level = sums[0:grid_rows].astype(BF16)
     level_ref[...] = level
     grads = sums[grid_rows : grid_rows + window]
@@ -551,6 +613,11 @@
         copy.wait_recv()
     mesh_sum = grads_ref[mesh_rows : 2 * mesh_rows] + halo_buf[0] + halo_buf[1]
     d_mesh_ref[...] = mm(mesh_sum.astype(BF16), w_send_ref[...], NT)
+    for part in parts:
+        part.s5()
+    vec_out_ref[...] = vec.total()
+    for part in parts:
+        part.s6()
     for copy in levels:
         copy.wait_recv()
     grid_sum = level_ref[span(x * share, share, 16), :].astype(F32)
@@ -558,17 +625,11 @@
         grid_sum = grid_sum + level_buf[d].astype(F32)
     d_grid_ref[...] = mm(grid_sum.astype(BF16), w_recv_ref[...], NT)
     for part in parts:
-        part.s5()
-    vec_out_ref[...] = vec.total()
-    for part in parts:
-        part.s6()
-    for part in parts:
         part.s7()
     for part in parts:
         part.s8()
     for part in parts:
         part.s9()
-    out[...] = total[...]
     copies.finish()
 
 
@@ -590,7 +651,6 @@
         in_specs=[vmem] * len(inputs),
         out_specs=(vmem,) * 4,
         scratch_shapes=[
-            comm[0],
             pltpu.VMEM((3 * width, width), BF16),
             pltpu.VMEM((grid_rows, width), BF16),
             pltpu.VMEM((4 * mesh_rows, width), F32),
@@ -598,6 +658,7 @@
             pltpu.VMEM((slots, width), F32),
             pltpu.VMEM((slots, width), BF16),
             pltpu.VMEM((slots, width), BF16),
+            *(pltpu.VMEM((BLOCK, width), BF16 if k in (1, 4) else F32) for k in range(6) for _ in range(2)),
             *comm[1:],
         ],
         compiler_params=pltpu.CompilerParams(

time: 74.3 us -> 69.1 us (0.930)
  Pallas kernels: 73.5 us -> 68.3 us
    pallas_call x1, Pallas kernels: 57.6 us -> 52.4 us  [main_call(): pl.pallas_call(main_kernel, out_shape=(jax.ShapeDtypeStruct((3 * width, w...]
where the time goes in v4:
time: 69.1 us; the launch traced here: 68.9 us
  Pallas kernels  68.3 us (99%)
    pallas_call x1, Pallas kernels, main_call(): pl.pallas_call(main_kernel, out_shape=(jax.ShapeDtypeStruct((3 * width, w...  52.4 us
    pallas_call x1, Pallas kernels, prep_call(): pl.pallas_call(prep_kernel, out_shape=outs, in_specs=[anywhere] * 11, out...  14.6 us

profile of v4, /device:TPU:1, one launch (start us, length us, event | category | flops | bytes accessed | tf_op | source)
XLA Modules:
  0.0 68.9 jit_solution(18017036291156689077)
XLA Ops:
  0.6 14.6 %shard_map.162 = (bf16[640,512]{1,0:T(8,128)(2,1)S(1)}, bf16[2048,640]{1,0:T(8,128)(2,1)S(1)}, bf16[640,2048]{1,0:T(8,128)(2,1)S(1)}, bf16[32,512]{1,0:T(8,128)(...) custom-call(bf16[512,512]{1,0:T(8,128)(2,1)} %grid_hbm.1, ...), custom_call_target="tpu_custom_call" | custom-call | tf_op jit(solution)/shard_map/pallas_call | solution.py:396
  15.3 52.4 %shard_map.163 = (bf16[1536,512]{1,0:T(8,128)(2,1)S(1)}, f32[2,512]{1,0:T(2,128)S(1)}, f32[128,512]{1,0:T(8,128)S(1)}, f32[8,512]{1,0:T(8,128)S(1)}) custom-call(bf16[640,512]{1,0:T(8,128)(2,1)S(1)} %get-tuple-element.29.table, bf16[2048,640]{1,0:T(8,128)(2,1)S(1)} %get-tuple-element.30.pick, bf16[640,2048]{1,0:T(8,128)(2,1)S(1)} %get-tuple-element.31.pick_t, ...), custom_call_target="tpu_custom_call" | custom-call | tf_op jit(solution)/shard_map/pallas_call | solution.py:643
  67.6 1.3 %shard_map.164 = (f32[128,512]{1,0:T(8,128)}, f32[8,512]{1,0:T(8,128)}, bf16[512,512]{1,0:T(8,128)(2,1)}, bf16[512,512]{1,0:T(8,128)(2,1)}, bf16[512,512]{1,0:T(...) custom-call(bf16[1536,512]{1,0:T(8,128)(2,1)S(1)} %get-tuple-element.40.total, f32[2,512]{1,0:T(2,128)S(1)} %get-tuple-element.41.vec, ...), custom_call_target="tpu_custom_call" | custom-call | tf_op jit(solution)/shard_map/pallas_call | solution.py:704
